TPU v7x, 16 devices: a whole 2x2x2 slice. The times are simulated.
16 devices in a mesh: dp: 2 (over z), sp: 8 (over y, x, core).
Axes of the slice: x: 2, y: 2, z: 2, core: 2. Of those that a mesh axis runs over, the one named last changes fastest.
Arguments:
- hidden: bfloat16 [12288, 2048], P(('dp', 'sp')), parts along dimension 0
- positions: int32 [12288], P(('dp', 'sp')), parts along dimension 0
- d_attn: bfloat16 [12288, 2048], P(('dp', 'sp')), parts along dimension 0
- ln_weight: bfloat16 [2048], replicated
- w_q: bfloat16 [2048, 2048], replicated
- w_k: bfloat16 [2048, 2048], replicated
- w_v: bfloat16 [2048, 2048], replicated
- w_o: bfloat16 [2048, 2048], replicated
Outputs:
- output 1: bfloat16 [12288, 2048], P(('dp', 'sp')), parts along dimension 0
- output 2: bfloat16 [12288, 2048], P(('dp', 'sp')), parts along dimension 0
- output 3: bfloat16 [4096], P('dp'), parts along dimension 0
- output 4: bfloat16 [4096, 2048], P('dp'), parts along dimension 0
- output 5: bfloat16 [4096, 2048], P('dp'), parts along dimension 0
- output 6: bfloat16 [4096, 2048], P('dp'), parts along dimension 0
- output 7: bfloat16 [4096, 2048], P('dp'), parts along dimension 0
There are 2 independent parts. A program takes and returns all parts, laid end to end along the dimension named above; an argument that names none is the same for every part.
All inputs are finite; a program needn't handle non-finite values.
Results may differ from a plain program's by a relative error of at most 0.0122763.
Values are sent between devices in bfloat16 or wider.
A program may use at most 1 GiB of HBM per device.

v0:
```python
import math
import jax
import jax.numpy as jnp
from jax import lax
from jax.sharding import PartitionSpec as P

HEAD_DIM = 128
LN_EPS = 1e-5
ROPE_BASE = 10000.0


def norm_f32(hid_f32, weight_f32):
    mean_val = jnp.mean(hid_f32, axis=-1, keepdims=True)
    centered = hid_f32 - mean_val
    var_val = jnp.mean(centered * centered, axis=-1, keepdims=True)
    return centered * lax.rsqrt(var_val + LN_EPS) * weight_f32


def rope_tables(positions):
    inv_freq = ROPE_BASE ** (-jnp.arange(0, HEAD_DIM, 2, dtype=jnp.float32) / HEAD_DIM)
    angles = positions.astype(jnp.float32)[:, None] * inv_freq[None, :]
    return jnp.cos(angles)[:, None, :], jnp.sin(angles)[:, None, :]


def apply_rope(values, cos_t, sin_t):
    rot_pairs = values.reshape(values.shape[:-1] + (HEAD_DIM // 2, 2))
    even_part = rot_pairs[..., 0]
    odd_part = rot_pairs[..., 1]
    new_even = even_part * cos_t - odd_part * sin_t
    new_odd = odd_part * cos_t + even_part * sin_t
    return jnp.stack([new_even, new_odd], axis=-1).reshape(values.shape)


def block_probs(q_block, row_start, k_all):
    scores = jnp.einsum('qgrd,kgd->grqk', q_block, k_all, preferred_element_type=jnp.float32) * (HEAD_DIM ** -0.5)
    row_ids = row_start + jnp.arange(q_block.shape[0])
    col_ids = jnp.arange(k_all.shape[0])
    scores = jnp.where(row_ids[:, None] >= col_ids[None, :], scores, -jnp.inf)
    return jax.nn.softmax(scores, axis=-1)


def attn_forward(q_grp, k_all, v_all, row_offset):
    n_rows = q_grp.shape[0]
    block_rows = math.gcd(n_rows, 128)
    q_blocks = q_grp.reshape((n_rows // block_rows, block_rows) + q_grp.shape[1:])

    def one_block(block_in):
        q_block, block_idx = block_in
        attn_prob = block_probs(q_block, row_offset + block_idx * block_rows, k_all)
        return jnp.einsum('grqk,kgd->qgrd', attn_prob.astype(jnp.bfloat16), v_all, preferred_element_type=jnp.float32).astype(jnp.bfloat16)

    o_blocks = lax.map(one_block, (q_blocks, jnp.arange(n_rows // block_rows)))
    return o_blocks.reshape(q_grp.shape)


def attn_backward(q_grp, k_all, v_all, do_grp, row_offset):
    n_rows = q_grp.shape[0]
    block_rows = math.gcd(n_rows, 128)
    block_shape = (n_rows // block_rows, block_rows) + q_grp.shape[1:]

    def one_block(carry, block_in):
        dk_acc, dv_acc = carry
        q_block, do_block, block_idx = block_in
        attn_prob = block_probs(q_block, row_offset + block_idx * block_rows, k_all)
        d_prob = jnp.einsum('qgrd,kgd->grqk', do_block, v_all, preferred_element_type=jnp.float32)
        row_dot = jnp.sum(attn_prob * d_prob, axis=-1, keepdims=True)
        d_score = (attn_prob * (d_prob - row_dot) * (HEAD_DIM ** -0.5)).astype(jnp.bfloat16)
        dq_block = jnp.einsum('grqk,kgd->qgrd', d_score, k_all, preferred_element_type=jnp.float32).astype(jnp.bfloat16)
        dk_acc = dk_acc + jnp.einsum('grqk,qgrd->kgd', d_score, q_block, preferred_element_type=jnp.float32)
        dv_acc = dv_acc + jnp.einsum('grqk,qgrd->kgd', attn_prob.astype(jnp.bfloat16), do_block, preferred_element_type=jnp.float32)
        return (dk_acc, dv_acc), dq_block

    zero_acc = jnp.zeros(k_all.shape, jnp.float32)
    kv_sums, dq_blocks = lax.scan(one_block, (zero_acc, zero_acc), (q_grp.reshape(block_shape), do_grp.reshape(block_shape), jnp.arange(block_shape[0])))
    return dq_blocks.reshape(q_grp.shape), kv_sums[0], kv_sums[1]


def solution(mesh):
    sp_size = mesh.shape['sp']
    row_spec = P(('dp', 'sp'), None)
    pos_spec = P(('dp', 'sp'))
    full_spec = P(None, None)
    grad_spec = P('dp', None)

    def local_step(hidden, positions, d_attn, ln_weight, w_q, w_k, w_v, w_o):
        local_rows = hidden.shape[0]
        n_heads = w_q.shape[1] // HEAD_DIM
        kv_heads = w_k.shape[1] // HEAD_DIM
        copies = max(sp_size // kv_heads, 1)
        normed32, norm_vjp = jax.vjp(norm_f32, hidden.astype(jnp.float32), ln_weight.astype(jnp.float32))
        normed = normed32.astype(jnp.bfloat16)
        cos_t, sin_t = rope_tables(positions)
        q_rot = apply_rope(jnp.dot(normed, w_q, preferred_element_type=jnp.float32).reshape(local_rows, n_heads, HEAD_DIM), cos_t, sin_t).astype(jnp.bfloat16)
        k_rot = apply_rope(jnp.dot(normed, w_k, preferred_element_type=jnp.float32).reshape(local_rows, kv_heads, HEAD_DIM), cos_t, sin_t).astype(jnp.bfloat16)
        v_loc = jnp.dot(normed, w_v, preferred_element_type=jnp.float32).astype(jnp.bfloat16).reshape(local_rows, kv_heads, HEAD_DIM)
        if copies > 1:
            k_rot = jnp.repeat(k_rot, copies, axis=1)
            v_loc = jnp.repeat(v_loc, copies, axis=1)
        q_heads = lax.all_to_all(q_rot, 'sp', 1, 0, tiled=True)
        k_heads = lax.all_to_all(k_rot, 'sp', 1, 0, tiled=True)
        v_heads = lax.all_to_all(v_loc, 'sp', 1, 0, tiled=True)
        seq_rows, heads_local = q_heads.shape[0], q_heads.shape[1]
        kv_local = k_heads.shape[1]
        q_grp = q_heads.reshape(seq_rows, kv_local, heads_local // kv_local, HEAD_DIM)
        o_grp = attn_forward(q_grp, k_heads, v_heads, 0)
        o_tok = lax.all_to_all(o_grp.reshape(q_heads.shape), 'sp', 0, 1, tiled=True).reshape(local_rows, n_heads * HEAD_DIM)
        attn_out = jnp.dot(o_tok, w_o, preferred_element_type=jnp.float32).astype(jnp.bfloat16)
        d_o = jnp.einsum('td,ed->te', d_attn, w_o, preferred_element_type=jnp.float32).astype(jnp.bfloat16)
        dw_o = jnp.einsum('te,td->ed', o_tok, d_attn, preferred_element_type=jnp.float32)
        do_heads = lax.all_to_all(d_o.reshape(local_rows, n_heads, HEAD_DIM), 'sp', 1, 0, tiled=True)
        dq_grp, dk_acc, dv_acc = attn_backward(q_grp, k_heads, v_heads, do_heads.reshape(q_grp.shape), 0)
        dq_tok = lax.all_to_all(dq_grp.reshape(q_heads.shape), 'sp', 0, 1, tiled=True)
        dk_tok = lax.all_to_all(dk_acc.astype(jnp.bfloat16), 'sp', 0, 1, tiled=True)
        dv_tok = lax.all_to_all(dv_acc.astype(jnp.bfloat16), 'sp', 0, 1, tiled=True)
        if copies > 1:
            dk_tok = dk_tok.reshape(local_rows, kv_heads, copies, HEAD_DIM).astype(jnp.float32).sum(axis=2).astype(jnp.bfloat16)
            dv_tok = dv_tok.reshape(local_rows, kv_heads, copies, HEAD_DIM).astype(jnp.float32).sum(axis=2).astype(jnp.bfloat16)
        g_q = apply_rope(dq_tok.astype(jnp.float32), cos_t, -sin_t).astype(jnp.bfloat16).reshape(local_rows, n_heads * HEAD_DIM)
        g_k = apply_rope(dk_tok.astype(jnp.float32), cos_t, -sin_t).astype(jnp.bfloat16).reshape(local_rows, kv_heads * HEAD_DIM)
        g_v = dv_tok.reshape(local_rows, kv_heads * HEAD_DIM)
        d_normed = (jnp.einsum('te,de->td', g_q, w_q, preferred_element_type=jnp.float32)
                    + jnp.einsum('te,de->td', g_k, w_k, preferred_element_type=jnp.float32)
                    + jnp.einsum('te,de->td', g_v, w_v, preferred_element_type=jnp.float32))
        dw_q = jnp.einsum('td,te->de', normed, g_q, preferred_element_type=jnp.float32)
        dw_k = jnp.einsum('td,te->de', normed, g_k, preferred_element_type=jnp.float32)
        dw_v = jnp.einsum('td,te->de', normed, g_v, preferred_element_type=jnp.float32)
        d_hid, d_lnw = norm_vjp(d_normed)
        grad_sums = lax.psum((d_lnw, dw_q, dw_k, dw_v, dw_o), 'sp')
        return (attn_out, d_hid.astype(jnp.bfloat16), grad_sums[0].astype(jnp.bfloat16), grad_sums[1].astype(jnp.bfloat16),
                grad_sums[2].astype(jnp.bfloat16), grad_sums[3].astype(jnp.bfloat16), grad_sums[4].astype(jnp.bfloat16))

    return jax.shard_map(local_step, mesh=mesh,
                         in_specs=(row_spec, pos_spec, row_spec, P(None), full_spec, full_spec, full_spec, full_spec),
                         out_specs=(row_spec, row_spec, P('dp'), grad_spec, grad_spec, grad_spec, grad_spec),
                         check_vma=False)
```

profile of v0, /device:TPU:0, one launch (start us, length us, event | category | flops | bytes accessed | tf_op | source)
XLA Modules:
  0.0 3317.0 jit_solution(14026696678400822720)
XLA Ops:
  5.2 9.3 fusion.51
  17.0 5.9 all-to-all-start.2
  22.9 9.1 fusion.52
  34.5 11.9 fusion.62
  46.4 8.1 reshape_reshape.21
  54.6 12.9 fusion.64
  67.5 8.1 reshape_reshape.19
  77.1 5.0 all-to-all-start.4
  82.1 19.2 subtract_convert_fusion.2
  101.3 15.2 pad_maximum_fusion
  122.5 4.6 all-to-all-start
  127.2 5.2 copy.94
  135.1 29.8 all-to-all-done
  164.9 4.5 all-to-all-start.1
  177.1 4.6 copy.92
  185.7 21.4 all-to-all-done.1
  207.1 4.6 copy.97
  214.2 1064.7 %while.26 = (s32[]{:T(128)}, f32[6144,2,128]{0,2,1:T(8,128)}, f32[6144,2,128]{0,2,1:T(8,128)}, bf16[48,128,2,1,128]{4,1,0,2,3:T(8,128)(2,1)}, bf16[48,128,2,1,12...) while((s32[]{:T(128)}, f32[6144,2,128]{0,2,1:T(8,128)}, ...), condition=%wide.region_10.11_spmd.clone, body=%wide.region_6.10_spmd.clone.sunk | while | flops 2048687488 | bytes 203239824 | solution.py:74
  1278.9 7.9 copy.110
  1291.3 9.7 copy.113
  1301.0 28.1 all-to-all-done.5
  1329.0 4.7 all-to-all-start.6
  1336.2 443.4 %while.25 = (s32[]{:T(128)}, bf16[48,128,2,1,128]{4,1,0,2,3:T(8,128)(2,1)}, s32[48]{0:T(128)S(1)}, bf16[48,128,2,1,128]{4,1,2,3,0:T(8,128)(2,1)}, bf16[6144,2,12...) while((s32[]{:T(128)}, bf16[48,128,2,1,128]{4,1,0,2,3:T(8,128)(2,1)}, ...), condition=%wide.region_5.6_spmd, body=%wide.region_2.5_spmd.sunk | while | flops 818708096 | bytes 39458972 | solution.py:52
  1779.6 7.9 copy.102
  1787.5 9.7 copy.115
  1802.8 6.6 copy.112
  1809.4 8.1 reshape.234
  1817.5 4.9 all-to-all-start.3
  1822.4 9.5 copy.114
  1831.9 8.2 reshape.235
  1840.1 19.4 subtract_convert_fusion
  1859.5 8.0 pad_maximum_fusion.3
  1867.5 7.5 convert_element_type.141
  1875.1 11.9 fusion.70
  1887.0 11.1 fusion.57
  1898.1 8.0 pad_maximum_fusion.2
  1906.1 7.5 convert_element_type.135
  1913.7 11.9 fusion.69
  1925.6 11.1 fusion.59
  1945.1 4.6 copy.104
  1949.7 12.1 convolution_convert_fusion.2
  1961.9 9.6 fusion.71
  1971.4 7.5 all-to-all-done.7
  1982.9 4.6 copy.117
  1987.5 13.2 fusion.55
  2000.7 17.2 fusion.48
  2017.9 4.9 fusion.66
  2024.8 1291.8 %all-reduce.2 = (bf16[2048]{0:T(1024)(128)(2,1)}, bf16[2048,2048]{1,0:T(8,128)(2,1)}, bf16[2048,2048]{1,0:T(8,128)(2,1)}, bf16[2048,2048]{1,0:T(8,128)(2,1)}, bf16[2048,2048]{1,0:T(8,128)(2,1)}) all-reduce(f32[2048]{0:T(1024)S(1)} %get-tuple-element.182, f32[2048,2048]{1,0:T(8,128)} %fusion.59, ...), channel_id=1, replica_groups=mesh['dp'=2,'sp'=8] {'sp'}, use_global_device_ids=true, to_apply=%region_14.15 | all-reduce | flops 16779264 | bytes 100675584 | tf_op jit(solution)/shard_map/psum | solution.py:128
  (1809 shorter events, 1502.5 us)
Async XLA Ops:
  0.6 22.2 copy-start
  3.6 50.9 %copy-start.20 = (f32[768]{0:T(1024)}, f32[768]{0:T(1024)S(1)}, u32[]{:S(2)}) copy-start(f32[768]{0:T(1024)S(1)} %broadcast_multiply_fusion) | copy-start | bytes 9220
  5.2 49.4 %copy-start.24 = (f32[768]{0:T(1024)}, f32[768]{0:T(1024)S(1)}, u32[]{:S(2)}) copy-start(f32[768]{0:T(1024)S(1)} %fusion.54) | copy-start | bytes 9220
  5.2 49.4 %copy-start.22 = (f32[2048]{0:T(1024)}, f32[2048]{0:T(1024)S(1)}, u32[]{:S(2)}) copy-start(f32[2048]{0:T(1024)S(1)} %convert_element_type.123) | copy-start | bytes 24580
  17.0 60.1 %all-to-all-start.2 = ((bf16[768,16,128]{2,0,1:T(8,128)(2,1)}), bf16[768,16,128]{2,0,1:T(8,128)(2,1)}, u32[]{:S(2)}, u32[]{:S(2)}) async-start(bf16[768,16,128]{2,0,1:T(8,128)(2,1)} %bitcast.224), calls=%async_computation.2 | async-start | bytes 6291456 | tf_op jit(solution)/shard_map/all_to_all | solution.py:101
  77.1 45.4 %all-to-all-start.4 = ((bf16[768,16,128]{2,0,1:T(8,128)(2,1)}), bf16[768,16,128]{2,0,1:T(8,128)(2,1)}, u32[]{:S(2)}, u32[]{:S(2)}) async-start(bf16[768,16,128]{2,0,1:T(8,128)(2,1)} %bitcast.223), calls=%async_computation.4 | async-start | bytes 6291456 | tf_op jit(solution)/shard_map/all_to_all | solution.py:110
  122.5 42.4 %all-to-all-start = ((bf16[768,16,128]{0,2,1:T(8,128)(2,1)}), bf16[768,16,128]{0,2,1:T(8,128)(2,1)}, u32[]{:S(2)}, u32[]{:S(2)}) async-start(bf16[768,16,128]{0,2,1:T(8,128)(2,1)} %copy.90), calls=%async_computation | async-start | bytes 6291456 | tf_op jit(solution)/shard_map/all_to_all | solution.py:99
  164.9 42.2 %all-to-all-start.1 = ((bf16[768,16,128]{0,2,1:T(8,128)(2,1)}), bf16[768,16,128]{0,2,1:T(8,128)(2,1)}, u32[]{:S(2)}, u32[]{:S(2)}) async-start(bf16[768,16,128]{0,2,1:T(8,128)(2,1)} %copy.95), calls=%async_computation.1 | async-start | bytes 6291456 | tf_op jit(solution)/shard_map/all_to_all | solution.py:100
  220.7 9.8 slice-start
  242.8 9.8 slice-start
  265.0 9.8 slice-start
  287.2 9.8 slice-start
  309.4 9.8 slice-start
  331.6 9.8 slice-start
  353.7 9.8 slice-start
  398.1 9.8 slice-start
  420.3 9.8 slice-start
  442.5 9.8 slice-start
  464.6 9.8 slice-start
  486.8 9.8 slice-start
  509.0 9.8 slice-start
  531.2 9.8 slice-start
  575.6 9.8 slice-start
  597.7 9.8 slice-start
  642.1 9.8 slice-start
  664.3 9.8 slice-start
  686.5 9.8 slice-start
  708.6 9.8 slice-start
  730.8 9.8 slice-start
  753.0 9.8 slice-start
  775.2 9.8 slice-start
  819.5 9.8 slice-start
  841.7 9.8 slice-start
  1286.8 42.2 %all-to-all-start.5 = ((bf16[6144,2,128]{2,1,0:T(2,128)(2,1)}), bf16[6144,2,128]{2,1,0:T(2,128)(2,1)}, u32[]{:S(2)}, u32[]{:S(2)}) async-start(bf16[6144,2,128]{2,1,0:T(2,128)(2,1)} %copy.110), calls=%async_computation.5 | async-start | bytes 6291456 | tf_op jit(solution)/shard_map/all_to_all | solution.py:112
  1329.0 488.5 %all-to-all-start.6 = ((bf16[6144,2,128]{2,1,0:T(2,128)(2,1)}), bf16[6144,2,128]{2,1,0:T(2,128)(2,1)}, u32[]{:S(2)}, u32[]{:S(2)}) async-start(bf16[6144,2,128]{2,1,0:T(2,128)(2,1)} %copy.113), calls=%async_computation.6 | async-start | bytes 6291456 | tf_op jit(solution)/shard_map/all_to_all | solution.py:113
  1817.5 119.1 %all-to-all-start.3 = ((bf16[6144,2,128]{2,1,0:T(2,128)(2,1)}), bf16[6144,2,128]{2,1,0:T(2,128)(2,1)}, u32[]{:S(2)}, u32[]{:S(2)}) async-start(bf16[6144,2,128]{2,1,0:T(2,128)(2,1)} %copy.102), calls=%async_computation.3 | async-start | bytes 6291456 | tf_op jit(solution)/shard_map/all_to_all | solution.py:106
  1875.0 11.9 copy-start.5
  1875.0 11.9 copy-start.12
  1875.0 11.9 copy-start.21
  1875.0 11.9 copy-start.23
  1875.0 11.9 copy-start.25
  1887.0 11.1 copy-start.7
  1887.0 11.1 copy-start.8
  1913.7 11.9 copy-start.6
  1913.7 11.9 copy-start.13
  1936.7 42.2 %all-to-all-start.7 = ((bf16[6144,2,128]{2,1,0:T(2,128)(2,1)}), bf16[6144,2,128]{2,1,0:T(2,128)(2,1)}, u32[]{:S(2)}, u32[]{:S(2)}) async-start(bf16[6144,2,128]{2,1,0:T(2,128)(2,1)} %copy.115), calls=%async_computation.7 | async-start | bytes 6291456 | tf_op jit(solution)/shard_map/all_to_all | solution.py:114
  1949.7 12.1 copy-start.14
  2000.7 17.2 copy-start.19
  (415 other events, 1663.5 us)
where the time goes:
time: 3330 us; the launch traced here: 3320 us
  blocking collectives  1290 us (39%)
  matrix products  1110 us (33%)
  local copies, waits for them, and re-layouts  397 us (12%)
  other arithmetic  323 us (10%)
  waiting for transfers between devices  86.8 us (3%)
  loops' own time  66.5 us (2%)
  starting transfers between devices  38.3 us (1%)
    psum x1, blocking collectives, local_step(): grad_sums = lax.psum((d_lnw, dw_q, dw_k, dw_v, dw_o), 'sp')  1290 us
    dot_general x96, matrix products, block_probs(): jnp.einsum('qgrd,kgd->grqk', q_block, k_all, preferred_element_type=jnp.f...  342 us
    while x864, local copies, waits for them, and re-layouts  177 us
    dot_general x48, matrix products, one_block(): jnp.einsum('grqk,qgrd->kgd', attn_prob.astype(jnp.bfloat16), do_block, pr...  157 us
    dot_general x48, matrix products, one_block(): jnp.einsum('grqk,qgrd->kgd', d_score, q_block, preferred_element_type=jnp...  155 us
    dot_general x48, matrix products, one_block(): jnp.einsum('qgrd,kgd->grqk', do_block, v_all, preferred_element_type=jnp....  134 us
    another operation x50, other arithmetic  130 us
    dot_general x48, matrix products, one_block(): jnp.einsum('grqk,kgd->qgrd', attn_prob.astype(jnp.bfloat16), v_all, prefe...  103 us
  transfers between devices with their start and end apart: 8, of which 4 were waited for; matrix products, arithmetic and copies ran while one was open for 21% of the time, Pallas kernels for 0%

commit v1 on v0

v1 whole, which is shorter than its diff:
```python
import functools
import math
import jax
import jax.numpy as jnp
from jax import lax
from jax.experimental import pallas as pl
from jax.experimental.pallas import tpu as pltpu
from jax.sharding import PartitionSpec as P

HEAD_DIM = 128
LN_EPS = 1e-5
ROPE_BASE = 10000.0
SCALE = HEAD_DIM ** -0.5
LOG2E = math.log2(math.e)
C2 = SCALE * LOG2E
NEG = -1e30
VLIM = 56 * 1024 * 1024
F32 = jnp.float32
BF16 = jnp.bfloat16


def norm_f32(hid_f32, weight_f32):
    mean_val = jnp.mean(hid_f32, axis=-1, keepdims=True)
    centered = hid_f32 - mean_val
    var_val = jnp.mean(centered * centered, axis=-1, keepdims=True)
    return centered * lax.rsqrt(var_val + LN_EPS) * weight_f32


def rope_tables(positions):
    lane = jnp.arange(HEAD_DIM)
    inv_freq = ROPE_BASE ** (-(lane - lane % 2).astype(F32) / HEAD_DIM)
    angles = positions.astype(F32)[:, None] * inv_freq[None, :]
    sign = jnp.where(lane % 2 == 0, -1.0, 1.0).astype(F32)
    return jnp.cos(angles), jnp.sin(angles) * sign[None, :]


def swap_pairs(val):
    lane = lax.broadcasted_iota(jnp.int32, val.shape, 1)
    return jnp.where(lane % 2 == 0, pltpu.roll(val, HEAD_DIM - 1, 1), pltpu.roll(val, 1, 1))


def rotate(val, cos_t, sin_t):
    return val * cos_t + swap_pairs(val) * sin_t


def dot_f32(lhs, rhs):
    return jnp.dot(lhs, rhs, preferred_element_type=F32)


def proj_kernel(heads, h_ref, w_ref, cos_ref, sin_ref, q_ref, k_ref, v_ref, qt_ref, kt_ref, vt_ref):
    cos_t, sin_t = cos_ref[...], sin_ref[...]
    width = heads * HEAD_DIM
    for idx, (out, out_t) in enumerate(((q_ref, qt_ref), (k_ref, kt_ref), (v_ref, vt_ref))):
        prod = dot_f32(h_ref[...], w_ref[:, idx * width:(idx + 1) * width])
        for n in range(heads):
            val = prod[:, n * HEAD_DIM:(n + 1) * HEAD_DIM]
            if idx < 2:
                val = rotate(val, cos_t, sin_t)
            out[n] = val.astype(BF16)
            out_t[n] = val.T.astype(BF16)


def project(h_all, w_cat, cos_t, sin_t, heads):
    rows, feat = h_all.shape
    width = w_cat.shape[1]
    bm = math.gcd(rows, 512)
    tok = pl.BlockSpec((heads, bm, HEAD_DIM), lambda i: (0, i, 0))
    tr = pl.BlockSpec((heads, HEAD_DIM, bm), lambda i: (0, 0, i))
    tab = pl.BlockSpec((bm, HEAD_DIM), lambda i: (i, 0))
    s_tok = jax.ShapeDtypeStruct((heads, rows, HEAD_DIM), BF16)
    s_tr = jax.ShapeDtypeStruct((heads, HEAD_DIM, rows), BF16)
    return pl.pallas_call(
        functools.partial(proj_kernel, heads), grid=(rows // bm,), name='qkv_proj',
        in_specs=[pl.BlockSpec((bm, feat), lambda i: (i, 0)), pl.BlockSpec((feat, width), lambda i: (0, 0)), tab, tab],
        out_specs=[tok] * 3 + [tr] * 3, out_shape=[s_tok] * 3 + [s_tr] * 3,
        compiler_params=pltpu.CompilerParams(vmem_limit_bytes=VLIM),
        cost_estimate=pl.CostEstimate(flops=2 * rows * feat * width, bytes_accessed=2 * rows * feat, transcendentals=0),
    )(h_all, w_cat, cos_t, sin_t)


def fwd_kernel(blk, k_ref, qt_ref, vt_ref, o_ref, ot_ref, lse_ref, acc_ref):
    qi = pl.program_id(1)
    qt = qt_ref[0]
    acc_ref[...] = jnp.zeros_like(acc_ref)

    def chunk(j, carry, masked):
        m_old, l_old = carry
        start = pl.multiple_of(j * blk, blk)
        s_t = dot_f32(k_ref[0, pl.ds(start, blk), :], qt)
        if masked:
            key = lax.broadcasted_iota(jnp.int32, s_t.shape, 0)
            qry = lax.broadcasted_iota(jnp.int32, s_t.shape, 1)
            s_t = jnp.where(key <= qry, s_t, NEG)
        m_new = jnp.maximum(m_old, jnp.max(s_t, axis=0, keepdims=True) * C2)
        p_t = jnp.exp2(s_t * C2 - m_new)
        alpha = jnp.exp2(m_old - m_new)
        l_new = l_old * alpha + jnp.sum(p_t, axis=0, keepdims=True)
        acc_ref[...] = acc_ref[...] * alpha + dot_f32(vt_ref[0, :, pl.ds(start, blk)], p_t.astype(BF16))
        return m_new, l_new

    init = (jnp.full((1, blk), NEG, F32), jnp.zeros((1, blk), F32))
    carry = lax.fori_loop(0, qi, lambda j, c: chunk(j, c, False), init)
    m_fin, l_fin = chunk(qi, carry, True)
    o_t = acc_ref[...] / l_fin
    ot_ref[0] = o_t
    o_ref[...] = o_t.T.astype(BF16)
    lse_ref[0] = m_fin + jnp.log2(l_fin)


def attn_fwd(k, q_t, v_t):
    heads, rows, _ = k.shape
    blk = math.gcd(rows, 512)
    full = pl.BlockSpec((1, rows, HEAD_DIM), lambda n, i: (n, 0, 0))
    full_t = pl.BlockSpec((1, HEAD_DIM, rows), lambda n, i: (n, 0, 0))
    blk_t = pl.BlockSpec((1, HEAD_DIM, blk), lambda n, i: (n, 0, i))
    return pl.pallas_call(
        functools.partial(fwd_kernel, blk), grid=(heads, rows // blk), name='attn_fwd',
        in_specs=[full, blk_t, full_t],
        out_specs=[pl.BlockSpec((blk, HEAD_DIM), lambda n, i: (i, n)), blk_t,
                   pl.BlockSpec((1, 1, blk), lambda n, i: (n, 0, i))],
        out_shape=[jax.ShapeDtypeStruct((rows, heads * HEAD_DIM), BF16),
                   jax.ShapeDtypeStruct((heads, HEAD_DIM, rows), F32),
                   jax.ShapeDtypeStruct((heads, 1, rows), F32)],
        scratch_shapes=[pltpu.VMEM((HEAD_DIM, blk), F32)],
        compiler_params=pltpu.CompilerParams(vmem_limit_bytes=VLIM),
        cost_estimate=pl.CostEstimate(flops=4 * heads * rows * rows * HEAD_DIM, bytes_accessed=8 * heads * rows * HEAD_DIM,
                                      transcendentals=heads * rows * rows // 2),
    )(k, q_t, v_t)


def do_kernel(heads, g_ref, wo_ref, ot_ref, do_ref, dot_ref, dsum_ref):
    prod = lax.dot_general(g_ref[...], wo_ref[...], (((1,), (1,)), ((), ())), preferred_element_type=F32)
    for n in range(heads):
        val = prod[:, n * HEAD_DIM:(n + 1) * HEAD_DIM].astype(BF16)
        val_t = val.astype(F32).T
        do_ref[n] = val
        dot_ref[n] = val_t.astype(BF16)
        dsum_ref[n] = jnp.sum(val_t * ot_ref[n], axis=0, keepdims=True)


def project_do(g_all, wo_rows, o_t, heads):
    rows, feat = g_all.shape
    width = wo_rows.shape[0]
    bm = math.gcd(rows, 512)
    tok = pl.BlockSpec((heads, bm, HEAD_DIM), lambda i: (0, i, 0))
    tr = pl.BlockSpec((heads, HEAD_DIM, bm), lambda i: (0, 0, i))
    return pl.pallas_call(
        functools.partial(do_kernel, heads), grid=(rows // bm,), name='do_proj',
        in_specs=[pl.BlockSpec((bm, feat), lambda i: (i, 0)), pl.BlockSpec((width, feat), lambda i: (0, 0)), tr],
        out_specs=[tok, tr, pl.BlockSpec((heads, 1, bm), lambda i: (0, 0, i))],
        out_shape=[jax.ShapeDtypeStruct((heads, rows, HEAD_DIM), BF16), jax.ShapeDtypeStruct((heads, HEAD_DIM, rows), BF16),
                   jax.ShapeDtypeStruct((heads, 1, rows), F32)],
        compiler_params=pltpu.CompilerParams(vmem_limit_bytes=VLIM),
        cost_estimate=pl.CostEstimate(flops=2 * rows * feat * width, bytes_accessed=2 * rows * feat, transcendentals=0),
    )(g_all, wo_rows, o_t)


def bwd_kernel(blk, n_blk, k_ref, v_ref, kt_ref, q_ref, qt_ref, do_ref, dot_ref, lse_ref, dsum_ref, cos_ref, sin_ref,
               gq_ref, gk_ref, gv_ref, dqt_ref, dk_ref, dv_ref):
    kj = pl.program_id(0)
    k_blk, v_blk, kt_blk = k_ref[0], v_ref[0], kt_ref[0]

    @pl.when(kj == 0)
    def _():
        dqt_ref[...] = jnp.zeros_like(dqt_ref)

    def chunk(i, masked):
        start = pl.multiple_of(i * blk, blk)
        cols = pl.ds(start, blk)
        p_t = jnp.exp2(dot_f32(k_blk, qt_ref[0, :, cols]) * C2 - lse_ref[0, :, cols])
        if masked:
            key = lax.broadcasted_iota(jnp.int32, p_t.shape, 0)
            qry = lax.broadcasted_iota(jnp.int32, p_t.shape, 1)
            p_t = jnp.where(key <= qry, p_t, 0.0)
        dp_t = dot_f32(v_blk, dot_ref[0, :, cols])
        ds_t = (p_t * ((dp_t - dsum_ref[0, :, cols]) * SCALE)).astype(BF16)
        dv_new = dot_f32(p_t.astype(BF16), do_ref[0, cols, :])
        dk_new = dot_f32(ds_t, q_ref[0, cols, :])
        if masked:
            dv_ref[...] = dv_new
            dk_ref[...] = dk_new
        else:
            dv_ref[...] += dv_new
            dk_ref[...] += dk_new
        dqt_ref[:, cols] += dot_f32(kt_blk, ds_t)

    chunk(kj, True)
    lax.fori_loop(kj + 1, n_blk, lambda i, c: (chunk(i, False), c)[1], 0)
    cos_t, sin_t = cos_ref[...], -sin_ref[...]
    own = pl.ds(pl.multiple_of(kj * blk, blk), blk)
    d_q = dqt_ref[:, own].T.astype(BF16).astype(F32)
    gq_ref[...] = rotate(d_q, cos_t, sin_t).astype(BF16)
    gk_ref[...] = rotate(dk_ref[...].astype(BF16).astype(F32), cos_t, sin_t).astype(BF16)
    gv_ref[...] = dv_ref[...].astype(BF16)


def attn_bwd(n, k, v, k_t, q, q_t, d_o, d_ot, lse, dsum, cos_t, sin_t):
    heads, rows, _ = k.shape
    blk = math.gcd(rows, 512)
    n_blk = rows // blk
    blk_tok = pl.BlockSpec((1, blk, HEAD_DIM), lambda j: (n, j, 0))
    blk_tr = pl.BlockSpec((1, HEAD_DIM, blk), lambda j: (n, 0, j))
    full = pl.BlockSpec((1, rows, HEAD_DIM), lambda j: (n, 0, 0))
    full_t = pl.BlockSpec((1, HEAD_DIM, rows), lambda j: (n, 0, 0))
    vec = pl.BlockSpec((1, 1, rows), lambda j: (n, 0, 0))
    tab = pl.BlockSpec((blk, HEAD_DIM), lambda j: (j, 0))
    return pl.pallas_call(
        functools.partial(bwd_kernel, blk, n_blk), grid=(n_blk,), name='attn_bwd',
        in_specs=[blk_tok, blk_tok, blk_tr, full, full_t, full, full_t, vec, vec, tab, tab],
        out_specs=[tab] * 3, out_shape=[jax.ShapeDtypeStruct((rows, HEAD_DIM), BF16)] * 3,
        scratch_shapes=[pltpu.VMEM((HEAD_DIM, rows), F32), pltpu.VMEM((blk, HEAD_DIM), F32), pltpu.VMEM((blk, HEAD_DIM), F32)],
        compiler_params=pltpu.CompilerParams(vmem_limit_bytes=VLIM),
        cost_estimate=pl.CostEstimate(flops=10 * rows * rows * HEAD_DIM, bytes_accessed=20 * rows * HEAD_DIM,
                                      transcendentals=rows * rows // 2),
    )(k, v, k_t, q, q_t, d_o, d_ot, lse, dsum, cos_t, sin_t)


def solution(mesh):
    sp_size = mesh.shape['sp']
    row_spec = P(('dp', 'sp'), None)
    pos_spec = P(('dp', 'sp'))
    full_spec = P(None, None)
    grad_spec = P('dp', None)

    def local_step(hidden, positions, d_attn, ln_weight, w_q, w_k, w_v, w_o):
        width = w_q.shape[1] // sp_size
        heads = width // HEAD_DIM
        me = lax.axis_index('sp')
        normed32, norm_vjp = jax.vjp(norm_f32, hidden.astype(F32), ln_weight.astype(F32))
        normed = normed32.astype(BF16)
        pos_all = lax.all_gather(positions, 'sp', axis=0, tiled=True)
        h_all = lax.all_gather(normed, 'sp', axis=0, tiled=True)
        g_dep, h_all = lax.optimization_barrier((d_attn, h_all))
        g_all = lax.all_gather(g_dep, 'sp', axis=0, tiled=True)
        cos_t, sin_t = rope_tables(pos_all)
        own = lambda w: lax.dynamic_slice_in_dim(w, me * width, width, 1)
        w_cat = jnp.concatenate([own(w_q), own(w_k), own(w_v)], axis=1)
        wo_rows = lax.dynamic_slice_in_dim(w_o, me * width, width, 0)
        q, k, v, q_t, k_t, v_t = project(h_all, w_cat, cos_t, sin_t, heads)
        o_tok, o_t, lse = attn_fwd(k, q_t, v_t)
        d_o, d_ot, dsum = project_do(g_all, wo_rows, o_t, heads)

        def to_owner(val):
            return lax.all_to_all(val, 'sp', 0, 1, tiled=True)

        def gather(grad, axis):
            return lax.all_gather(grad, 'sp', axis=axis, tiled=True)

        o_own = to_owner(o_tok)
        attn_out = dot_f32(o_own, w_o).astype(BF16)
        dw_o = gather(jnp.einsum('te,td->ed', o_tok, g_all, preferred_element_type=F32).astype(BF16), 0)
        parts = [attn_bwd(n, k, v, k_t, q, q_t, d_o, d_ot, lse, dsum, cos_t, sin_t) for n in range(heads)]
        grads = []
        d_normed = 0.0
        for idx, w in enumerate((w_q, w_k, w_v)):
            g_tok = jnp.concatenate([part[idx] for part in parts], axis=1)
            d_w = jnp.einsum('td,te->de', h_all, g_tok, preferred_element_type=F32).astype(BF16)
            grads.append(gather(d_w, 1))
            d_normed = d_normed + jnp.einsum('te,de->td', to_owner(g_tok), w, preferred_element_type=F32)
        d_hid, d_lnw = norm_vjp(d_normed)
        d_lnw = lax.psum(d_lnw, 'sp')
        return (attn_out, d_hid.astype(BF16), d_lnw.astype(BF16), grads[0], grads[1], grads[2], dw_o)

    return jax.shard_map(local_step, mesh=mesh,
                         in_specs=(row_spec, pos_spec, row_spec, P(None), full_spec, full_spec, full_spec, full_spec),
                         out_specs=(row_spec, row_spec, P('dp'), grad_spec, grad_spec, grad_spec, grad_spec),
                         check_vma=False)
```

time: 3330 us -> 842 us (0.25)
  blocking collectives: 1290 us -> 21.9 us
  matrix products: 1110 us -> 106 us
  local copies, waits for them, and re-layouts: 397 us -> 63.9 us
  Pallas kernels: 0 us -> 307 us
  other arithmetic: 323 us -> 27.7 us
  waiting for transfers between devices: 86.8 us -> 273 us
  loops' own time: 66.5 us -> 0 us
    psum x1, blocking collectives: 1290 us -> 12.9 us  [local_step(): d_lnw = lax.psum(d_lnw, 'sp')]
    dot_general x348 -> x8, matrix products: 1110 us -> 106 us  [the longest x3 40.7 us: local_step(): jnp.einsum('te,de->td', to_owner(g_tok), w, preferred_element_type=F32)]
    pallas_call x0 -> x5, Pallas kernels: none -> 307 us  [the longest x2 141 us: attn_bwd(): pl.pallas_call(functools.partial(bwd_kernel, blk, n_blk), grid=(n_blk,),...]
    while x867 -> x0, local copies, waits for them, and re-layouts: 200 us -> none
    another operation x53 -> x0, other arithmetic: 161 us -> none
    all_gather x0 -> x6, waiting for transfers between devices: none -> 124 us  [the longest x1 124 us: local_step(): h_all = lax.all_gather(normed, 'sp', axis=0, tiled=True)]
    reduce_sum x96 -> x0, other arithmetic: 97.4 us -> none  [block_probs(): return jax.nn.softmax(scores, axis=-1)]
    another operation x2 -> x0, loops' own time: 66.5 us -> none  [the longest x1 34 us: attn_backward(): lax.scan(one_block, (zero_acc, zero_acc), (q_grp.reshape(block_shape), do...]
  transfers between devices with their start and end apart: 8 -> 10, of which waited for: 4 -> 5; matrix products, arithmetic and copies ran while one was open for 21% -> 16% of each run, Pallas kernels for 0% -> 37%
where the time goes in v1:
time: 842 us; the launch traced here: 833 us
  Pallas kernels  307 us (36%)
  waiting for transfers between devices  273 us (32%)
  matrix products  106 us (13%)
  local copies, waits for them, and re-layouts  63.9 us (8%)
  other arithmetic  27.7 us (3%)
  blocking collectives  21.9 us (3%)
  starting transfers between devices  19 us (2%)
  between operations  14.9 us (2%)
    all_to_all x4, waiting for transfers between devices, to_owner(): return lax.all_to_all(val, 'sp', 0, 1, tiled=True)  148 us
    pallas_call x2, Pallas kernels, attn_bwd(): pl.pallas_call(functools.partial(bwd_kernel, blk, n_blk), grid=(n_blk,),...  141 us
    all_gather x1, waiting for transfers between devices, local_step(): h_all = lax.all_gather(normed, 'sp', axis=0, tiled=True)  124 us
    pallas_call x1, Pallas kernels, attn_fwd(): pl.pallas_call(functools.partial(fwd_kernel, blk), grid=(heads, rows // b...  115 us
    unnamed x54, local copies, waits for them, and re-layouts  45 us
    dot_general x3, matrix products, local_step(): jnp.einsum('te,de->td', to_owner(g_tok), w, preferred_element_type=F32)  40.7 us
    dot_general x3, matrix products, local_step(): jnp.einsum('td,te->de', h_all, g_tok, preferred_element_type=F32)  39.7 us
    pallas_call x1, Pallas kernels, project(): pl.pallas_call(functools.partial(proj_kernel, heads), grid=(rows // bm,),...  31 us
  transfers between devices with their start and end apart: 10, of which 5 were waited for; matrix products, arithmetic and copies ran while one was open for 16% of the time, Pallas kernels for 37%

profile of v1, /device:TPU:0, one launch (start us, length us, event | category | flops | bytes accessed | tf_op | source)
XLA Modules:
  0.0 833.2 jit_solution(6429456680187858080)
XLA Ops:
  7.2 2.5 convert_reduce_fusion
  10.0 1.0 fusion.8
  12.8 2.7 fusion.6
  15.5 124.4 %all-gather.8.cloned.1.call-done.h_ref = bf16[6144,2048]{1,0:T(8,128)(2,1)} async-done(((bf16[768,2048]{1,0:T(8,128)(2,1)}), bf16[6144,2048]{1,0:T(8,128)(2,1)}) %all-gather.8.cloned.1.call-update) | async-done | bytes 25165840 | tf_op jit(solution)/shard_map/all_gather | solution.py:232
  140.0 8.9 %all-gather = s32[8,1,768]{2,1,0:T(1,128)S(1)} all-gather(s32[1,1,768]{2,1,0:T(1,128)S(1)} %reshape.74), channel_id=1, replica_groups=mesh['dp'=2,'sp'=8] {'sp'}, dimensions={0}, use_global_device_ids=true | all-gather | bytes 27648 | tf_op jit(solution)/shard_map/all_gather | solution.py:231
  149.0 1.3 constant_dynamic-slice_fusion.3
  150.3 1.7 constant_dynamic-slice_fusion.1
  152.0 1.8 pad_maximum_fusion.w_ref
  153.8 13.6 %fusion.10 = (f32[6144,128]{1,0:T(8,128)}, f32[6144,128]{1,0:T(8,128)}) fusion(f32[128]{0:T(128)S(1)} %get-tuple-element.54, f32[128]{0:T(128)S(1)} %get-tuple-element.55, f32[6144]{0:T(1024)S(1)} %bitcast.37), kind=kLoop, calls=%fused_computation.18 | loop fusion | flops 1572864 | bytes 6317056 | tf_op jit(solution)/shard_map/mul | solution.py:34
  167.4 31.0 %qkv_proj.1 = (bf16[2,6144,128]{2,1,0:T(8,128)(2,1)}, bf16[2,6144,128]{2,1,0:T(8,128)(2,1)}, bf16[2,6144,128]{2,1,0:T(8,128)(2,1)}, bf16[2,128,6144]{2,1,0:T(8,1...) custom-call(bf16[6144,2048]{1,0:T(8,128)(2,1)} %all-gather.8.cloned.1.call-done.h_ref, ...), custom_call_target="tpu_custom_call" | custom-call | flops 19327352832 | bytes 25165824 | tf_op jit(solution)/shard_map/qkv_proj/pallas_call | solution.py:72
  198.3 114.9 %attn_fwd.1 = (bf16[6144,256]{1,0:T(8,128)(2,1)}, f32[2,128,6144]{2,1,0:T(8,128)}, f32[2,1,6144]{2,1,0:T(1,128)}) custom-call(bf16[2,6144,128]{2,1,0:T(8,128)(2,1)} %get-tuple-element.28.k_ref, bf16[2,128,6144]{2,1,0:T(8,128)(2,1)} %get-tuple-element.29.qt_ref, bf16[2,128,6144]{2,1,0:T(8,128)(2,1)} %get-tuple-element.30.vt_ref), custom_call_target="tpu_custom_call" | custom-call | flops 38654705664 | bytes 12582912 | tf_op jit(solution)/shard_map/attn_fwd/pallas_call | solution.py:116
  313.3 13.4 %convolution_convert_fusion.4 = bf16[256,2048]{1,0:T(8,128)(2,1)} fusion(bf16[6144,256]{1,0:T(8,128)(2,1)} %get-tuple-element.31, bf16[6144,2048]{1,0:T(8,128)(2,1)} %all-gather.10.cloned.1.call-done.g_ref), kind=kOutput, calls=%fused_computation.23 | convolution fusion | flops 6442975232 | bytes 29360128 | tf_op jit(solution)/shard_map/te,td->ed/dot_general | solution.py:251
  327.2 2.3 constant_dynamic-slice_fusion.wo_ref
  329.5 20.0 %do_proj.1 = (bf16[2,6144,128]{2,1,0:T(8,128)(2,1)}, bf16[2,128,6144]{2,1,0:T(8,128)(2,1)}, f32[2,1,6144]{2,1,0:T(1,128)}) custom-call(bf16[6144,2048]{1,0:T(8,128)(2,1)} %all-gather.10.cloned.1.call-done.g_ref, bf16[256,2048]{1,0:T(8,128)(2,1)} %constant_dynamic-slice_fusion.wo_ref, f32[2,128,6144]{2,1,0:T(8,128)} %get-tuple-element.36.ot_ref), custom_call_target="tpu_custom_call" | custom-call | flops 6442450944 | bytes 25165824 | tf_op jit(solution)/shard_map/do_proj/pallas_call | solution.py:147
  349.5 70.6 %attn_bwd.2 = (bf16[6144,128]{1,0:T(8,128)(2,1)}, bf16[6144,128]{1,0:T(8,128)(2,1)}, bf16[6144,128]{1,0:T(8,128)(2,1)}) custom-call(bf16[2,6144,128]{2,1,0:T(8,128)(2,1)} %get-tuple-element.28.k_ref, bf16[2,6144,128]{2,1,0:T(8,128)(2,1)} %get-tuple-element.32.v_ref, bf16[2,128,6144]{2,1,0:T(8,128)(2,1)} %get-tuple-element.33.kt_ref, ...), custom_call_target="tpu_custom_call" | custom-call | flops 48318382080 | bytes 15728640 | tf_op jit(solution)/shard_map/attn_bwd/pallas_call | solution.py:207
  420.1 1.7 constant_dynamic-update-slice_fusion.1
  421.8 70.6 %attn_bwd.3 = (bf16[6144,128]{1,0:T(8,128)(2,1)}, bf16[6144,128]{1,0:T(8,128)(2,1)}, bf16[6144,128]{1,0:T(8,128)(2,1)}) custom-call(bf16[2,6144,128]{2,1,0:T(8,128)(2,1)} %get-tuple-element.28.k_ref, bf16[2,6144,128]{2,1,0:T(8,128)(2,1)} %get-tuple-element.32.v_ref, bf16[2,128,6144]{2,1,0:T(8,128)(2,1)} %get-tuple-element.33.kt_ref, ...), custom_call_target="tpu_custom_call" | custom-call | flops 48318382080 | bytes 15728640 | tf_op jit(solution)/shard_map/attn_bwd/pallas_call | solution.py:207
  492.4 1.8 constant_dynamic-update-slice_fusion
  494.2 1.7 copy-done.3
  495.9 13.2 %convolution_convert_fusion.3 = bf16[2048,256]{1,0:T(8,128)(2,1)} fusion(bf16[6144,2048]{1,0:T(8,128)(2,1)} %all-gather.8.cloned.1.call-done.h_ref, bf16[6144,256]{1,0:T(8,128)(2,1)S(1)} %constant_dynamic-update-slice_fusion), kind=kOutput, calls=%fused_computation.22 | convolution fusion | flops 6442975232 | bytes 29360128 | tf_op jit(solution)/shard_map/td,te->de/dot_general | solution.py:257
  510.8 1.7 copy-done.7
  512.5 13.2 %convolution_convert_fusion.2 = bf16[2048,256]{1,0:T(8,128)(2,1)} fusion(bf16[6144,2048]{1,0:T(8,128)(2,1)} %all-gather.8.cloned.1.call-done.h_ref, bf16[6144,256]{1,0:T(8,128)(2,1)S(1)} %constant_dynamic-update-slice_fusion.2), kind=kOutput, calls=%fused_computation.21 | convolution fusion | flops 6442975232 | bytes 29360128 | tf_op jit(solution)/shard_map/td,te->de/dot_general | solution.py:257
  525.8 2.8 copy.19
  528.5 4.6 all-to-all-start
  533.5 1.1 copy-done.10
  534.9 1.7 copy-done.5
  536.6 13.3 %convolution_convert_fusion.1 = bf16[2048,256]{1,0:T(8,128)(2,1)} fusion(bf16[6144,2048]{1,0:T(8,128)(2,1)} %all-gather.8.cloned.1.call-done.h_ref, bf16[6144,256]{1,0:T(8,128)(2,1)S(1)} %constant_dynamic-update-slice_fusion.4), kind=kOutput, calls=%fused_computation.20 | convolution fusion | flops 6442975232 | bytes 29360128 | tf_op jit(solution)/shard_map/td,te->de/dot_general | solution.py:257
  549.9 2.8 copy.20
  552.6 39.6 %all-to-all-done = bf16[8,768,256]{1,2,0:T(8,128)(2,1)} async-done(((bf16[8,768,256]{1,2,0:T(8,128)(2,1)}), bf16[8,768,256]{1,2,0:T(8,128)(2,1)}, u32[]{:S(2)}, u32[]{:S(2)}) %all-to-all-start) | async-done | bytes 3145760 | tf_op jit(solution)/shard_map/all_to_all | solution.py:244
  592.2 4.5 all-to-all-start.1
  596.7 2.8 copy.21
  599.5 46.2 %all-to-all-done.1 = bf16[8,768,256]{1,2,0:T(8,128)(2,1)} async-done(((bf16[8,768,256]{1,2,0:T(8,128)(2,1)}), bf16[8,768,256]{1,2,0:T(8,128)(2,1)}, u32[]{:S(2)}, u32[]{:S(2)}) %all-to-all-start.1) | async-done | bytes 3145760 | tf_op jit(solution)/shard_map/all_to_all | solution.py:244
  645.7 4.5 all-to-all-start.2
  650.1 12.1 %convolution_convert_fusion = bf16[768,2048]{1,0:T(8,128)(2,1)} fusion(bf16[768,2048]{0,1:T(8,128)(2,1)} %bitcast.3, bf16[2048,2048]{1,0:T(8,128)(2,1)} %param.15), kind=kOutput, calls=%fused_computation.17 | convolution fusion | flops 6444023808 | bytes 14680064 | tf_op jit(solution)/shard_map/dot_general | solution.py:47
  662.3 2.8 copy.22
  665.0 37.3 %all-to-all-done.2 = bf16[8,768,256]{1,2,0:T(8,128)(2,1)} async-done(((bf16[8,768,256]{1,2,0:T(8,128)(2,1)}), bf16[8,768,256]{1,2,0:T(8,128)(2,1)}, u32[]{:S(2)}, u32[]{:S(2)}) %all-to-all-start.2) | async-done | bytes 3145760 | tf_op jit(solution)/shard_map/all_to_all | solution.py:244
  702.3 4.7 all-to-all-start.3
  707.0 11.8 %fusion.17 = f32[768,2048]{1,0:T(8,128)} fusion(bf16[768,2048]{0,1:T(8,128)(2,1)} %bitcast.6, bf16[2048,2048]{1,0:T(8,128)(2,1)} %param.12), kind=kOutput, calls=%fused_computation.48 | convolution fusion | flops 6442450944 | bytes 17825792 | tf_op jit(solution)/shard_map/te,de->td/dot_general | solution.py:259
  718.8 11.9 %fusion.18 = f32[768,2048]{1,0:T(8,128)} fusion(bf16[768,2048]{0,1:T(8,128)(2,1)} %bitcast.9, bf16[2048,2048]{1,0:T(8,128)(2,1)} %param.13), kind=kOutput, calls=%fused_computation.49 | convolution fusion | flops 6442450944 | bytes 17825792 | tf_op jit(solution)/shard_map/te,de->td/dot_general | solution.py:259
  730.7 25.3 %all-to-all-done.3 = bf16[8,768,256]{1,2,0:T(8,128)(2,1)} async-done(((bf16[8,768,256]{1,2,0:T(8,128)(2,1)}), bf16[8,768,256]{1,2,0:T(8,128)(2,1)}, u32[]{:S(2)}, u32[]{:S(2)}) %all-to-all-start.3) | async-done | bytes 3145760 | tf_op jit(solution)/shard_map/all_to_all | solution.py:244
  756.0 17.1 %fusion.7 = (f32[2048]{0:T(1024)S(1)}, f32[768]{0:T(1024)S(1)}, f32[768,2048]{1,0:T(8,128)}) fusion(bf16[768,2048]{1,0:T(8,128)(2,1)S(1)} %copy-done.1, f32[768]{0:T(1024)S(1)} %copy-done.20, f32[768]{0:T(1024)S(1)} %copy-done.16, f32[2048]{0:T(1024)S(1)} %copy-done.14, bf16[768,2048]{0,1:T(8,128)(2,1)} %bitcast.12, bf16[2048,2048]{1,0:T(8,128)(2,1)} %param.14, ...), kind=kOutput, calls=%fused_computation.10 | convolution fusion | flops 6458176512 | bytes 33580032 | tf_op jit(solution)/shard_map/te,de->td/dot_general | solution.py:259
  773.1 12.9 %psum.7 = bf16[2048]{0:T(1024)(128)(2,1)} all-reduce(f32[2048]{0:T(1024)S(1)} %get-tuple-element.47), channel_id=1, replica_groups=mesh['dp'=2,'sp'=8] {'sp'}, use_global_device_ids=true, to_apply=%region_5.6 | all-reduce | flops 2048 | bytes 12288 | tf_op jit(solution)/shard_map/psum | solution.py:261
  786.0 4.1 fusion.16
  790.1 2.1 add_convert_fusion
  792.2 8.4 %copy.30 = bf16[2048,2048]{1,0:T(8,128)(2,1)} copy(bf16[2048,2048]{1,0:T(8,128)(2,1)} %all-gather.12.cloned.1.call-done) | data formatting | bytes 16777216
  800.6 8.4 %copy.31 = bf16[2048,2048]{1,0:T(8,128)(2,1)} copy(bf16[2048,2048]{1,0:T(8,128)(2,1)} %all-gather.14.cloned.1.call-done) | data formatting | bytes 16777216
  809.1 8.4 %copy.32 = bf16[2048,2048]{1,0:T(8,128)(2,1)} copy(bf16[2048,2048]{1,0:T(8,128)(2,1)} %all-gather.16.cloned.1.call-done) | data formatting | bytes 16777216
  817.5 8.4 %copy.33 = bf16[2048,2048]{1,0:T(8,128)(2,1)} copy(bf16[2048,2048]{1,0:T(8,128)(2,1)} %all-gather.18.cloned.1.call-done) | data formatting | bytes 16777216
  (71 shorter events, 5.3 us)
Async XLA Ops:
  7.2 2.8 copy-start
  7.2 4.4 copy-start.21
  7.2 132.7 %all-gather.8.cloned.1.call-start = ((), (), s32[]{:S(2)}) async-start(), calls=%async_computation.4 | async-start | bytes 28311552 | tf_op jit(solution)/shard_map/all_gather | solution.py:232
  10.0 1.6 copy-start.15
  11.0 0.6 copy-start.17
  11.6 0.6 copy-start.19
  12.2 0.6 copy-start.13
  15.4 124.5 %copy-start.22 = (s32[768]{0:T(1024)S(1)}, s32[768]{0:T(1024)}, u32[]{:S(2)}) copy-start(s32[768]{0:T(1024)} %param.9) | copy-start | bytes 9220
  15.5 297.8 %all-gather.10.cloned.1.call-start = ((), (), s32[]{:S(2)}) async-start(), calls=%async_computation.5 | async-start | bytes 28311552 | tf_op jit(solution)/shard_map/all_gather | solution.py:234
  139.9 652.2 %all-gather.18.cloned.1.call-start = ((), (), s32[]{:S(2)}) async-start(), calls=%async_computation.9 | async-start | bytes 9437184 | tf_op jit(solution)/shard_map/all_gather | solution.py:247
  326.7 465.5 %all-gather.12.cloned.1.call-start = ((), (), s32[]{:S(2)}) async-start(), calls=%async_computation.6 | async-start | bytes 9437184 | tf_op jit(solution)/shard_map/all_gather | solution.py:247
  494.2 1.7 copy-start.3
  495.9 13.4 %copy-start.11 = (bf16[6144,128]{1,0:T(8,128)(2,1)S(1)}, bf16[6144,128]{1,0:T(8,128)(2,1)}, u32[]{:S(2)}) copy-start(bf16[6144,128]{1,0:T(8,128)(2,1)} %get-tuple-element.43) | copy-start | bytes 4718596
  509.0 1.4 copy-start.12
  509.1 283.1 %all-gather.14.cloned.1.call-start = ((), (), s32[]{:S(2)}) async-start(), calls=%async_computation.7 | async-start | bytes 9437184 | tf_op jit(solution)/shard_map/all_gather | solution.py:247
  510.8 1.7 copy-start.7
  512.5 13.3 %copy-start.2 = (bf16[6144,256]{1,0:T(8,128)(2,1)S(1)}, bf16[6144,256]{1,0:T(8,128)(2,1)}, u32[]{:S(2)}) copy-start(bf16[6144,256]{1,0:T(8,128)(2,1)} %get-tuple-element.31) | copy-start | bytes 9437188
  528.5 4.7 copy-start.9
  528.5 63.7 %all-to-all-start = ((bf16[8,768,256]{1,2,0:T(8,128)(2,1)}), bf16[8,768,256]{1,2,0:T(8,128)(2,1)}, u32[]{:S(2)}, u32[]{:S(2)}) async-start(bf16[8,768,256]{1,2,0:T(8,128)(2,1)} %copy.19), calls=%async_computation | async-start | bytes 6291456 | tf_op jit(solution)/shard_map/all_to_all | solution.py:244
  533.1 1.4 copy-start.10
  533.1 259.0 %all-gather.16.cloned.1.call-start = ((), (), s32[]{:S(2)}) async-start(), calls=%async_computation.8 | async-start | bytes 9437184 | tf_op jit(solution)/shard_map/all_gather | solution.py:247
  534.9 1.7 copy-start.5
  536.6 13.3 %copy-start.4 = (bf16[6144,256]{1,0:T(8,128)(2,1)S(1)}, bf16[6144,256]{1,0:T(8,128)(2,1)}, u32[]{:S(2)}) copy-start(bf16[6144,256]{1,0:T(8,128)(2,1)} %copy-done.3) | copy-start | bytes 9437188
  552.6 44.1 %copy-start.8 = (bf16[6144,256]{1,0:T(8,128)(2,1)S(1)}, bf16[6144,256]{1,0:T(8,128)(2,1)}, u32[]{:S(2)}) copy-start(bf16[6144,256]{1,0:T(8,128)(2,1)} %copy-done.7) | copy-start | bytes 9437188
  592.2 53.4 %all-to-all-start.1 = ((bf16[8,768,256]{1,2,0:T(8,128)(2,1)}), bf16[8,768,256]{1,2,0:T(8,128)(2,1)}, u32[]{:S(2)}, u32[]{:S(2)}) async-start(bf16[8,768,256]{1,2,0:T(8,128)(2,1)} %copy.20), calls=%async_computation.1 | async-start | bytes 6291456 | tf_op jit(solution)/shard_map/all_to_all | solution.py:244
  645.7 56.7 %all-to-all-start.2 = ((bf16[8,768,256]{1,2,0:T(8,128)(2,1)}), bf16[8,768,256]{1,2,0:T(8,128)(2,1)}, u32[]{:S(2)}, u32[]{:S(2)}) async-start(bf16[8,768,256]{1,2,0:T(8,128)(2,1)} %copy.21), calls=%async_computation.2 | async-start | bytes 6291456 | tf_op jit(solution)/shard_map/all_to_all | solution.py:244
  650.1 12.1 %copy-start.6 = (bf16[6144,256]{1,0:T(8,128)(2,1)S(1)}, bf16[6144,256]{1,0:T(8,128)(2,1)}, u32[]{:S(2)}) copy-start(bf16[6144,256]{1,0:T(8,128)(2,1)} %copy-done.5) | copy-start | bytes 9437188
  702.3 53.6 %all-to-all-start.3 = ((bf16[8,768,256]{1,2,0:T(8,128)(2,1)}), bf16[8,768,256]{1,2,0:T(8,128)(2,1)}, u32[]{:S(2)}, u32[]{:S(2)}) async-start(bf16[8,768,256]{1,2,0:T(8,128)(2,1)} %copy.22), calls=%async_computation.3 | async-start | bytes 6291456 | tf_op jit(solution)/shard_map/all_to_all | solution.py:244
  718.8 37.2 %copy-start.1 = (bf16[768,2048]{1,0:T(8,128)(2,1)S(1)}, bf16[768,2048]{1,0:T(8,128)(2,1)}, u32[]{:S(2)}) copy-start(bf16[768,2048]{1,0:T(8,128)(2,1)} %param.8) | copy-start | bytes 9437188
  718.8 37.2 %copy-start.14 = (f32[2048]{0:T(1024)S(1)}, f32[2048]{0:T(1024)}, u32[]{:S(2)}) copy-start(f32[2048]{0:T(1024)} %copy-done.13) | copy-start | bytes 24580
  718.8 37.2 %copy-start.16 = (f32[768]{0:T(1024)S(1)}, f32[768]{0:T(1024)}, u32[]{:S(2)}) copy-start(f32[768]{0:T(1024)} %copy-done.15) | copy-start | bytes 9220
  718.8 37.2 %copy-start.20 = (f32[768]{0:T(1024)S(1)}, f32[768]{0:T(1024)}, u32[]{:S(2)}) copy-start(f32[768]{0:T(1024)} %copy-done.19) | copy-start | bytes 9220
  756.0 30.0 %copy-start.18 = (f32[768]{0:T(1024)S(1)}, f32[768]{0:T(1024)}, u32[]{:S(2)}) copy-start(f32[768]{0:T(1024)} %copy-done.17) | copy-start | bytes 9220
Sparse Core Ops, SparseCore 0:
  15.6 124.2 all-gather.7
  141.7 121.4 all-gather.9
  326.8 50.1 all-gather.17
  509.2 77.0 all-gather.11
  588.5 106.2 all-gather.13
  696.5 85.2 all-gather.15

commit v2 on v1

v2 whole, which is shorter than its diff:
```python
import functools
import math
import jax
import jax.numpy as jnp
from jax import lax
from jax.experimental import pallas as pl
from jax.experimental.layout import Layout, with_layout_constraint
from jax.experimental.pallas import tpu as pltpu
from jax.sharding import PartitionSpec as P

HEAD_DIM = 128
LN_EPS = 1e-5
ROPE_BASE = 10000.0
SCALE = HEAD_DIM ** -0.5
LOG2E = math.log2(math.e)
C2 = SCALE * LOG2E
NEG = -1e30
VLIM = 56 * 1024 * 1024
F32 = jnp.float32
BF16 = jnp.bfloat16


def norm_f32(hid_f32, weight_f32):
    mean_val = jnp.mean(hid_f32, axis=-1, keepdims=True)
    centered = hid_f32 - mean_val
    var_val = jnp.mean(centered * centered, axis=-1, keepdims=True)
    return centered * lax.rsqrt(var_val + LN_EPS) * weight_f32


def norm_kernel(x_ref, w_ref, out_ref):
    out_ref[...] = norm_f32(x_ref[...].astype(F32), w_ref[...].astype(F32)).astype(BF16)


def layer_norm(hidden, weight):
    rows, feat = hidden.shape
    bm = math.gcd(rows, 256)
    spec = pl.BlockSpec((bm, feat), lambda i: (i, 0))
    return pl.pallas_call(
        norm_kernel, grid=(rows // bm,), name='layer_norm',
        in_specs=[spec, pl.BlockSpec((1, feat), lambda i: (0, 0))], out_specs=spec,
        out_shape=jax.ShapeDtypeStruct((rows, feat), BF16),
        cost_estimate=pl.CostEstimate(flops=10 * rows * feat, bytes_accessed=4 * rows * feat, transcendentals=rows),
    )(hidden, weight[None, :])


def rope_tables(positions):
    lane = jnp.arange(HEAD_DIM)
    inv_freq = ROPE_BASE ** (-(lane - lane % 2).astype(F32) / HEAD_DIM)
    angles = positions.astype(F32)[:, None] * inv_freq[None, :]
    sign = jnp.where(lane % 2 == 0, -1.0, 1.0).astype(F32)
    return jnp.cos(angles), jnp.sin(angles) * sign[None, :]


def swap_pairs(val):
    lane = lax.broadcasted_iota(jnp.int32, val.shape, 1)
    return jnp.where(lane % 2 == 0, pltpu.roll(val, HEAD_DIM - 1, 1), pltpu.roll(val, 1, 1))


def rotate(val, cos_t, sin_t):
    return val * cos_t + swap_pairs(val) * sin_t


def dot_f32(lhs, rhs):
    return jnp.dot(lhs, rhs, preferred_element_type=F32)


def proj_kernel(heads, h_ref, w_ref, cos_ref, sin_ref, q_ref, k_ref, v_ref, qt_ref, kt_ref, vt_ref):
    cos_t, sin_t = cos_ref[...], sin_ref[...]
    width = heads * HEAD_DIM
    for idx, (out, out_t) in enumerate(((q_ref, qt_ref), (k_ref, kt_ref), (v_ref, vt_ref))):
        prod = dot_f32(h_ref[...], w_ref[:, idx * width:(idx + 1) * width])
        for n in range(heads):
            val = prod[:, n * HEAD_DIM:(n + 1) * HEAD_DIM]
            if idx < 2:
                val = rotate(val, cos_t, sin_t)
            val = val.astype(BF16)
            out[n] = val
            out_t[n] = val.T


def project(h_all, w_cat, cos_t, sin_t, heads):
    rows, feat = h_all.shape
    width = w_cat.shape[1]
    bm = math.gcd(rows, 512)
    tok = pl.BlockSpec((heads, bm, HEAD_DIM), lambda i: (0, i, 0))
    tr = pl.BlockSpec((heads, HEAD_DIM, bm), lambda i: (0, 0, i))
    tab = pl.BlockSpec((bm, HEAD_DIM), lambda i: (i, 0))
    s_tok = jax.ShapeDtypeStruct((heads, rows, HEAD_DIM), BF16)
    s_tr = jax.ShapeDtypeStruct((heads, HEAD_DIM, rows), BF16)
    return pl.pallas_call(
        functools.partial(proj_kernel, heads), grid=(rows // bm,), name='qkv_proj',
        in_specs=[pl.BlockSpec((bm, feat), lambda i: (i, 0)), pl.BlockSpec((feat, width), lambda i: (0, 0)), tab, tab],
        out_specs=[tok] * 3 + [tr] * 3, out_shape=[s_tok] * 3 + [s_tr] * 3,
        compiler_params=pltpu.CompilerParams(vmem_limit_bytes=VLIM),
        cost_estimate=pl.CostEstimate(flops=2 * rows * feat * width, bytes_accessed=2 * rows * feat, transcendentals=0),
    )(h_all, w_cat, cos_t, sin_t)


def fwd_kernel(blk, heads, k_ref, qt_ref, vt_ref, o_ref, ot_ref, lse_ref, acc_ref):
    qi = pl.program_id(0)
    acc_ref[...] = jnp.zeros_like(acc_ref)

    def chunk(j, carry, masked):
        start = pl.multiple_of(j * blk, blk)
        scores = [dot_f32(k_ref[n, pl.ds(start, blk), :], qt_ref[n]) for n in range(heads)]
        if masked:
            key = lax.broadcasted_iota(jnp.int32, (blk, blk), 0)
            qry = lax.broadcasted_iota(jnp.int32, (blk, blk), 1)
            scores = [jnp.where(key <= qry, s_t, NEG) for s_t in scores]
        out = []
        for n in range(heads):
            m_old, l_old = carry[n]
            s_t = scores[n]
            m_new = jnp.maximum(m_old, jnp.max(s_t, axis=0, keepdims=True) * C2)
            p_t = jnp.exp2(s_t * C2 - m_new)
            alpha = jnp.exp2(m_old - m_new)
            l_new = l_old * alpha + jnp.sum(p_t, axis=0, keepdims=True)
            acc_ref[n] = acc_ref[n] * alpha + dot_f32(vt_ref[n, :, pl.ds(start, blk)], p_t.astype(BF16))
            out.append((m_new, l_new))
        return tuple(out)

    init = tuple((jnp.full((1, blk), NEG, F32), jnp.zeros((1, blk), F32)) for _ in range(heads))
    carry = lax.fori_loop(0, qi, lambda j, c: chunk(j, c, False), init)
    carry = chunk(qi, carry, True)
    for n in range(heads):
        m_fin, l_fin = carry[n]
        o_t = acc_ref[n] / l_fin
        ot_ref[n] = o_t
        o_ref[:, n * HEAD_DIM:(n + 1) * HEAD_DIM] = o_t.T.astype(BF16)
        lse_ref[n] = m_fin + jnp.log2(l_fin)


def attn_fwd(k, q_t, v_t):
    heads, rows, _ = k.shape
    blk = math.gcd(rows, 768)
    full = pl.BlockSpec((heads, rows, HEAD_DIM), lambda i: (0, 0, 0))
    full_t = pl.BlockSpec((heads, HEAD_DIM, rows), lambda i: (0, 0, 0))
    blk_t = pl.BlockSpec((heads, HEAD_DIM, blk), lambda i: (0, 0, i))
    return pl.pallas_call(
        functools.partial(fwd_kernel, blk, heads), grid=(rows // blk,), name='attn_fwd',
        in_specs=[full, blk_t, full_t],
        out_specs=[pl.BlockSpec((blk, heads * HEAD_DIM), lambda i: (i, 0)), blk_t,
                   pl.BlockSpec((heads, 1, blk), lambda i: (0, 0, i))],
        out_shape=[jax.ShapeDtypeStruct((rows, heads * HEAD_DIM), BF16),
                   jax.ShapeDtypeStruct((heads, HEAD_DIM, rows), F32),
                   jax.ShapeDtypeStruct((heads, 1, rows), F32)],
        scratch_shapes=[pltpu.VMEM((heads, HEAD_DIM, blk), F32)],
        compiler_params=pltpu.CompilerParams(vmem_limit_bytes=VLIM),
        cost_estimate=pl.CostEstimate(flops=4 * heads * rows * rows * HEAD_DIM, bytes_accessed=8 * heads * rows * HEAD_DIM,
                                      transcendentals=heads * rows * rows // 2),
    )(k, q_t, v_t)


def do_kernel(heads, g_ref, wo_ref, ot_ref, do_ref, dot_ref, dsum_ref, dwo_ref, acc_ref):
    step = pl.program_id(0)

    @pl.when(step == 0)
    def _():
        acc_ref[...] = jnp.zeros_like(acc_ref)

    prod = dot_f32(g_ref[...], wo_ref[...])
    for n in range(heads):
        own = slice(n * HEAD_DIM, (n + 1) * HEAD_DIM)
        val = prod[:, own].astype(BF16)
        val_t = val.T
        o_t = ot_ref[n]
        do_ref[n] = val
        dot_ref[n] = val_t
        dsum_ref[n] = jnp.sum(val_t.astype(F32) * o_t, axis=0, keepdims=True)
        acc_ref[own, :] += dot_f32(o_t.astype(BF16), g_ref[...])

    @pl.when(step == pl.num_programs(0) - 1)
    def _():
        dwo_ref[...] = acc_ref[...].astype(BF16)


def project_do(g_all, wo_cols, o_t, heads):
    rows, feat = g_all.shape
    width = wo_cols.shape[1]
    bm = math.gcd(rows, 1024)
    tok = pl.BlockSpec((heads, bm, HEAD_DIM), lambda i: (0, i, 0))
    tr = pl.BlockSpec((heads, HEAD_DIM, bm), lambda i: (0, 0, i))
    return pl.pallas_call(
        functools.partial(do_kernel, heads), grid=(rows // bm,), name='do_dwo',
        in_specs=[pl.BlockSpec((bm, feat), lambda i: (i, 0)), pl.BlockSpec((feat, width), lambda i: (0, 0)), tr],
        out_specs=[tok, tr, pl.BlockSpec((heads, 1, bm), lambda i: (0, 0, i)), pl.BlockSpec((width, feat), lambda i: (0, 0))],
        out_shape=[jax.ShapeDtypeStruct((heads, rows, HEAD_DIM), BF16), jax.ShapeDtypeStruct((heads, HEAD_DIM, rows), BF16),
                   jax.ShapeDtypeStruct((heads, 1, rows), F32), jax.ShapeDtypeStruct((width, feat), BF16)],
        scratch_shapes=[pltpu.VMEM((width, feat), F32)],
        compiler_params=pltpu.CompilerParams(vmem_limit_bytes=VLIM),
        cost_estimate=pl.CostEstimate(flops=4 * rows * feat * width, bytes_accessed=2 * rows * feat, transcendentals=0),
    )(g_all, wo_cols, o_t)


def bwd_kernel(blk, n_blk, k_ref, v_ref, kt_ref, q_ref, qt_ref, do_ref, dot_ref, lse_ref, dsum_ref, cos_ref, sin_ref,
               g_ref, dqt_ref, dk_ref, dv_ref):
    kj = pl.program_id(0)
    half = blk // 2

    @pl.when(kj == 0)
    def _():
        dqt_ref[...] = jnp.zeros_like(dqt_ref)

    def tile(k_lo, k_num, q_start, q_num, masked, first):
        keys = slice(k_lo, k_lo + k_num)
        cols = pl.ds(q_start, q_num)
        p_t = jnp.exp2(dot_f32(k_ref[0, keys, :], qt_ref[0, :, cols]) * C2 - lse_ref[0, :, cols])
        if masked:
            key = lax.broadcasted_iota(jnp.int32, p_t.shape, 0)
            qry = lax.broadcasted_iota(jnp.int32, p_t.shape, 1)
            p_t = jnp.where(key <= qry, p_t, 0.0)
        dp_t = dot_f32(v_ref[0, keys, :], dot_ref[0, :, cols])
        ds_t = (p_t * ((dp_t - dsum_ref[0, :, cols]) * SCALE)).astype(BF16)
        dv_new = dot_f32(p_t.astype(BF16), do_ref[0, cols, :])
        dk_new = dot_f32(ds_t, q_ref[0, cols, :])
        if first:
            dv_ref[keys, :] = dv_new
            dk_ref[keys, :] = dk_new
        else:
            dv_ref[keys, :] += dv_new
            dk_ref[keys, :] += dk_new
        dqt_ref[:, cols] += dot_f32(kt_ref[0, :, keys], ds_t)

    base = pl.multiple_of(kj * blk, blk)
    tile(0, half, base, half, True, True)
    tile(half, half, base + half, half, True, True)
    tile(0, half, base + half, half, False, False)

    def body(i, carry):
        tile(0, blk, pl.multiple_of(i * blk, blk), blk, False, False)
        return carry

    lax.fori_loop(kj + 1, n_blk, body, 0)
    cos_t, sin_t = cos_ref[...], -sin_ref[...]
    d_q = dqt_ref[:, pl.ds(base, blk)].T.astype(BF16).astype(F32)
    g_ref[:, :HEAD_DIM] = rotate(d_q, cos_t, sin_t).astype(BF16)
    g_ref[:, HEAD_DIM:2 * HEAD_DIM] = rotate(dk_ref[...].astype(BF16).astype(F32), cos_t, sin_t).astype(BF16)
    g_ref[:, 2 * HEAD_DIM:] = dv_ref[...].astype(BF16)


def attn_bwd(n, k, v, k_t, q, q_t, d_o, d_ot, lse, dsum, cos_t, sin_t):
    _, rows, _ = k.shape
    blk = math.gcd(rows, 1024)
    n_blk = rows // blk
    blk_tok = pl.BlockSpec((1, blk, HEAD_DIM), lambda j: (n, j, 0))
    blk_tr = pl.BlockSpec((1, HEAD_DIM, blk), lambda j: (n, 0, j))
    full = pl.BlockSpec((1, rows, HEAD_DIM), lambda j: (n, 0, 0))
    full_t = pl.BlockSpec((1, HEAD_DIM, rows), lambda j: (n, 0, 0))
    vec = pl.BlockSpec((1, 1, rows), lambda j: (n, 0, 0))
    tab = pl.BlockSpec((blk, HEAD_DIM), lambda j: (j, 0))
    return pl.pallas_call(
        functools.partial(bwd_kernel, blk, n_blk), grid=(n_blk,), name='attn_bwd',
        in_specs=[blk_tok, blk_tok, blk_tr, full, full_t, full, full_t, vec, vec, tab, tab],
        out_specs=pl.BlockSpec((blk, 3 * HEAD_DIM), lambda j: (j, 0)),
        out_shape=jax.ShapeDtypeStruct((rows, 3 * HEAD_DIM), BF16),
        scratch_shapes=[pltpu.VMEM((HEAD_DIM, rows), F32), pltpu.VMEM((blk, HEAD_DIM), F32), pltpu.VMEM((blk, HEAD_DIM), F32)],
        compiler_params=pltpu.CompilerParams(vmem_limit_bytes=VLIM),
        cost_estimate=pl.CostEstimate(flops=10 * rows * rows * HEAD_DIM, bytes_accessed=20 * rows * HEAD_DIM,
                                      transcendentals=rows * rows // 2),
    )(k, v, k_t, q, q_t, d_o, d_ot, lse, dsum, cos_t, sin_t)


def copy_kernel(a_ref, out_ref):
    out_ref[...] = a_ref[...]


def copy_rows(val):
    rows, feat = val.shape
    spec = pl.BlockSpec((math.gcd(rows, 256), feat), lambda i: (i, 0))
    return pl.pallas_call(
        copy_kernel, grid=(rows // spec.block_shape[0],), name='copy_rows', in_specs=[spec], out_specs=spec,
        out_shape=jax.ShapeDtypeStruct(val.shape, val.dtype),
        cost_estimate=pl.CostEstimate(flops=rows * feat, bytes_accessed=4 * rows * feat, transcendentals=0),
    )(val)


def place_kernel(a_ref, *refs):
    for idx, out in enumerate(refs[-3:]):
        out[...] = a_ref[0, :, idx * HEAD_DIM:(idx + 1) * HEAD_DIM]


def place_slot(n, heads, gathered, grads):
    devs, feat, width = gathered.shape
    spec = pl.BlockSpec((feat, HEAD_DIM), lambda j: (0, j * heads + n))
    shape = jax.ShapeDtypeStruct((feat, devs * heads * HEAD_DIM), BF16)
    return pl.pallas_call(
        place_kernel, grid=(devs,), name='place',
        in_specs=[pl.BlockSpec((1, feat, width), lambda j: (j, 0, 0))] + [pl.BlockSpec(memory_space=pl.ANY)] * len(grads),
        out_specs=[spec] * 3, out_shape=[shape] * 3,
        input_output_aliases={1 + i: i for i in range(len(grads))},
        compiler_params=pltpu.CompilerParams(vmem_limit_bytes=VLIM),
        cost_estimate=pl.CostEstimate(flops=devs * feat * width, bytes_accessed=4 * devs * feat * width, transcendentals=0),
    )(gathered, *grads)


def solution(mesh):
    sp_size = mesh.shape['sp']
    row_spec = P(('dp', 'sp'), None)
    pos_spec = P(('dp', 'sp'))
    full_spec = P(None, None)
    grad_spec = P('dp', None)

    def layer_step(hidden, positions, d_attn, ln_weight, w_q, w_k, w_v, w_o):
        feat, all_width = w_q.shape
        width = all_width // sp_size
        heads = width // HEAD_DIM
        me = lax.axis_index('sp')
        normed = layer_norm(hidden, ln_weight)
        pos_all = lax.all_gather(positions, 'sp', axis=0, tiled=True)
        h_all = lax.all_gather(normed, 'sp', axis=0, tiled=True)
        cos_t, sin_t = rope_tables(pos_all)
        own = lambda w: lax.dynamic_slice_in_dim(w, me * width, width, 1)
        w_cat = jnp.concatenate([own(w_q), own(w_k), own(w_v)], axis=1)
        wo_cols = lax.dynamic_slice_in_dim(w_o, me * width, width, 0).T
        stacked = jnp.stack([w.reshape(feat, sp_size, heads, HEAD_DIM) for w in (w_q, w_k, w_v)], axis=3)
        w_slot = [stacked[:, :, n].reshape(feat, sp_size * 3 * HEAD_DIM) for n in range(heads)]
        h_all, cos_t, sin_t, w_cat, wo_cols, w_slot = lax.optimization_barrier((h_all, cos_t, sin_t, w_cat, wo_cols, w_slot))
        g_dep, h_all = lax.optimization_barrier((d_attn, h_all))
        g_all = lax.all_gather(g_dep, 'sp', axis=0, tiled=True)
        q, k, v, q_t, k_t, v_t = project(h_all, w_cat, cos_t, sin_t, heads)
        o_tok, o_t, lse = attn_fwd(k, q_t, v_t)

        row_major = Layout(major_to_minor=(0, 1, 2))

        def to_owner(val):
            val = with_layout_constraint(val.reshape(sp_size, -1, val.shape[1]), row_major)
            val = with_layout_constraint(lax.all_to_all(val, 'sp', 0, 0, tiled=True), row_major)
            return val.transpose(1, 0, 2).reshape(val.shape[1], -1)

        o_tok, g_all = lax.optimization_barrier((o_tok, g_all))
        o_own = to_owner(o_tok)
        d_o, d_ot, dsum, dw_o = project_do(g_all, wo_cols, o_t, heads)
        dw_o = lax.all_gather(dw_o, 'sp', axis=0, tiled=True)
        dw_o = copy_rows(dw_o)
        attn_out = dot_f32(o_own, w_o).astype(BF16)
        d_ws = []
        d_normed = 0.0
        for n in range(heads):
            g_tok = attn_bwd(n, k, v, k_t, q, q_t, d_o, d_ot, lse, dsum, cos_t, sin_t)
            g_own = to_owner(g_tok)
            d_w = jnp.einsum('td,te->de', h_all, g_tok, preferred_element_type=F32).astype(BF16)
            d_ws.append(lax.all_gather(d_w, 'sp', axis=0))
            d_normed = d_normed + jnp.einsum('te,de->td', g_own, w_slot[n], preferred_element_type=F32)
        grads = ()
        for n in range(heads):
            grads = place_slot(n, heads, d_ws[n], grads)
        norm_vjp = jax.vjp(norm_f32, hidden.astype(F32), ln_weight.astype(F32))[1]
        d_hid, d_lnw = norm_vjp(d_normed)
        d_lnw = lax.psum(d_lnw, 'sp')
        return (attn_out, d_hid.astype(BF16), d_lnw.astype(BF16), grads[0], grads[1], grads[2], dw_o)

    return jax.shard_map(layer_step, mesh=mesh,
                         in_specs=(row_spec, pos_spec, row_spec, P(None), full_spec, full_spec, full_spec, full_spec),
                         out_specs=(row_spec, row_spec, P('dp'), grad_spec, grad_spec, grad_spec, grad_spec),
                         check_vma=False)
```

time: 842 us -> 755 us (0.90)
  waiting for transfers between devices: 273 us -> 66 us
  blocking collectives: 21.9 us -> 172 us
  Pallas kernels: 307 us -> 281 us
  matrix products: 106 us -> 84.3 us
  local copies, waits for them, and re-layouts: 63.9 us -> 83.2 us
  other arithmetic: 27.7 us -> 42.6 us
  starting transfers between devices: 19 us -> 6.38 us
    all_to_all x0 -> x2, blocking collectives: none -> 148 us  [to_owner(): lax.all_to_all(val, 'sp', 0, 0, tiled=True)]
    all_to_all x4 -> x1, waiting for transfers between devices: 148 us -> 30 us  [to_owner(): lax.all_to_all(val, 'sp', 0, 0, tiled=True)]
    all_gather x6 -> x5, waiting for transfers between devices: 124 us -> 35.9 us  [the longest x1 21.4 us: layer_step(): g_all = lax.all_gather(g_dep, 'sp', axis=0, tiled=True)]
    dot_general x7 -> x4, matrix products: 93.8 us -> 72.3 us  [the longest x2 40.6 us: layer_step(): jnp.einsum('td,te->de', h_all, g_tok, preferred_element_type=F32)]
    slice x0 -> x3, local copies, waits for them, and re-layouts: none -> 21.3 us  [layer_step(): stacked[:, :, n].reshape(feat, sp_size * 3 * HEAD_DIM)]
    pallas_call x2, Pallas kernels: 141 us -> 121 us  [attn_bwd(): pl.pallas_call(functools.partial(bwd_kernel, blk, n_blk), grid=(n_blk,),...]
    another operation x0 -> x1, other arithmetic: none -> 19.6 us  [layer_step(): jnp.stack([w.reshape(feat, sp_size, heads, HEAD_DIM) for w in (w_q, w_k,...]
    transpose x0 -> x3, local copies, waits for them, and re-layouts: none -> 17.9 us  [to_owner(): return val.transpose(1, 0, 2).reshape(val.shape[1], -1)]
  transfers between devices with their start and end apart: 10 -> 6, of which waited for: 5 -> 3; matrix products, arithmetic and copies ran while one was open for 16% -> 28% of each run, Pallas kernels for 37% -> 33%
where the time goes in v2:
time: 755 us; the launch traced here: 749 us
  Pallas kernels  281 us (37%)
  blocking collectives  172 us (23%)
  matrix products  84.3 us (11%)
  local copies, waits for them, and re-layouts  83.2 us (11%)
  waiting for transfers between devices  66 us (9%)
  other arithmetic  42.6 us (6%)
  between operations  14.1 us (2%)
    all_to_all x2, blocking collectives, to_owner(): lax.all_to_all(val, 'sp', 0, 0, tiled=True)  148 us
    pallas_call x2, Pallas kernels, attn_bwd(): pl.pallas_call(functools.partial(bwd_kernel, blk, n_blk), grid=(n_blk,),...  121 us
    pallas_call x1, Pallas kernels, attn_fwd(): pl.pallas_call(functools.partial(fwd_kernel, blk, heads), grid=(rows // b...  69.2 us
    dot_general x2, matrix products, layer_step(): jnp.einsum('td,te->de', h_all, g_tok, preferred_element_type=F32)  40.6 us
    unnamed x17, local copies, waits for them, and re-layouts  38.2 us
    pallas_call x1, Pallas kernels, project(): pl.pallas_call(functools.partial(proj_kernel, heads), grid=(rows // bm,),...  32.2 us
    dot_general x2, matrix products, layer_step(): jnp.einsum('te,de->td', g_own, w_slot[n], preferred_element_type=F32)  31.7 us
    all_to_all x1, waiting for transfers between devices, to_owner(): lax.all_to_all(val, 'sp', 0, 0, tiled=True)  30 us
  transfers between devices with their start and end apart: 6, of which 3 were waited for; matrix products, arithmetic and copies ran while one was open for 28% of the time, Pallas kernels for 33%

profile of v2, /device:TPU:0, one launch (start us, length us, event | category | flops | bytes accessed | tf_op | source)
XLA Modules:
  0.0 748.8 jit_solution(4695701552241525125)
XLA Ops:
  7.2 0.0 all-gather.9.cloned.1.call-start
  7.2 1.3 broadcast_in_dim.23.w_ref
  8.5 5.2 layer_norm.1
  13.7 0.0 all-gather.11.cloned.1.call-start
  13.8 10.8 %all-gather.2 = s32[8,1,768]{2,1,0:T(1,128)S(1)} all-gather(s32[1,1,768]{2,1,0:T(1,128)S(1)} %reshape.88), channel_id=1, replica_groups=mesh['dp'=2,'sp'=8] {'sp'}, dimensions={0}, use_global_device_ids=true | all-gather | bytes 27648 | tf_op jit(solution)/shard_map/all_gather | solution.py:309
  24.6 1.5 constant_dynamic-slice_fusion
  26.1 1.3 copy.41
  27.4 12.4 %copy.33 = bf16[2048,2048]{0,1:T(8,128)(2,1)} copy(bf16[2048,2048]{1,0:T(8,128)(2,1)} %param.12) | data formatting | bytes 16777216 | tf_op args[4]
  39.8 12.2 %copy.34 = bf16[2048,2048]{0,1:T(8,128)(2,1)} copy(bf16[2048,2048]{1,0:T(8,128)(2,1)} %param.13) | data formatting | bytes 16777216 | tf_op args[5]
  52.0 12.2 %copy.35 = bf16[2048,2048]{0,1:T(8,128)(2,1)} copy(bf16[2048,2048]{1,0:T(8,128)(2,1)} %param.14) | data formatting | bytes 16777216 | tf_op args[6]
  64.3 19.6 %pad_maximum_fusion = bf16[2048,8,2,3,128]{0,4,2,1,3:T(8,128)(2,1)} fusion(bf16[2048,8,2,1,128]{0,4,2,1,3:T(8,128)(2,1)} %bitcast.30, bf16[2048,8,2,1,128]{0,4,2,1,3:T(8,128)(2,1)} %bitcast.29, bf16[2048,8,2,1,128]{0,4,2,1,3:T(8,128)(2,1)} %bitcast.28), kind=kLoop, calls=%fused_computation | loop fusion | flops 25165824 | bytes 50331648 | tf_op jit(solution)/shard_map/stack | solution.py:315
  83.8 10.3 %fusion.15 = (bf16[2048,8,1,3,128]{0,4,2,1,3:T(8,128)(2,1)S(1)}, bf16[2048,8,1,3,128]{0,4,2,1,3:T(8,128)(2,1)S(1)}) fusion(bf16[2048,8,2,3,128]{0,4,2,1,3:T(8,128)(2,1)} %pad_maximum_fusion), kind=kLoop, calls=%fused_computation.39 | loop fusion | bytes 50331648 | tf_op jit(solution)/shard_map/slice | solution.py:316
  94.1 5.5 copy.37
  99.7 5.5 copy.36
  105.2 1.3 constant_dynamic-slice_fusion.3
  106.5 1.7 constant_dynamic-slice_fusion.1
  108.2 1.8 pad_maximum_fusion.1.w_ref
  110.0 13.6 %fusion.8 = (f32[6144,128]{1,0:T(8,128)}, f32[6144,128]{1,0:T(8,128)}) fusion(f32[128]{0:T(128)S(1)} %get-tuple-element.76, f32[128]{0:T(128)S(1)} %get-tuple-element.77, f32[6144]{0:T(1024)S(1)} %bitcast.44), kind=kLoop, calls=%fused_computation.17 | loop fusion | flops 1572864 | bytes 6317056 | tf_op jit(solution)/shard_map/mul | solution.py:51
  123.6 14.5 %all-gather.9.cloned.1.call-done.h_ref = bf16[6144,2048]{1,0:T(8,128)(2,1)} async-done(((bf16[768,2048]{1,0:T(8,128)(2,1)}), bf16[6144,2048]{1,0:T(8,128)(2,1)}) %all-gather.9.cloned.1.call-update) | async-done | bytes 25165840 | tf_op jit(solution)/shard_map/all_gather | solution.py:310
  138.1 0.6 all-gather.13.cloned.1.call-start
  138.7 32.2 %qkv_proj.1 = (bf16[2,6144,128]{2,1,0:T(8,128)(2,1)}, bf16[2,6144,128]{2,1,0:T(8,128)(2,1)}, bf16[2,6144,128]{2,1,0:T(8,128)(2,1)}, bf16[2,128,6144]{2,1,0:T(8,1...) custom-call(bf16[6144,2048]{1,0:T(8,128)(2,1)} %all-gather.9.cloned.1.call-done.h_ref, ...), custom_call_target="tpu_custom_call" | custom-call | flops 19327352832 | bytes 25165824 | tf_op jit(solution)/shard_map/qkv_proj/pallas_call | solution.py:90
  170.9 69.2 %attn_fwd.1 = (bf16[6144,256]{1,0:T(8,128)(2,1)}, f32[2,128,6144]{2,1,0:T(8,128)}, f32[2,1,6144]{2,1,0:T(1,128)}) custom-call(bf16[2,6144,128]{2,1,0:T(8,128)(2,1)} %get-tuple-element.42.k_ref, bf16[2,128,6144]{2,1,0:T(8,128)(2,1)} %get-tuple-element.43.qt_ref, bf16[2,128,6144]{2,1,0:T(8,128)(2,1)} %get-tuple-element.44.vt_ref), custom_call_target="tpu_custom_call" | custom-call | flops 38654705664 | bytes 12582912 | tf_op jit(solution)/shard_map/attn_fwd/pallas_call | solution.py:139
  240.0 21.4 %all-gather.11.cloned.1.call-done.g_ref = bf16[6144,2048]{1,0:T(8,128)(2,1)} async-done(((bf16[768,2048]{1,0:T(8,128)(2,1)}), bf16[6144,2048]{1,0:T(8,128)(2,1)}) %all-gather.11.cloned.1.call-update) | async-done | bytes 25165840 | tf_op jit(solution)/shard_map/all_gather | solution.py:319
  261.4 20.0 %do_dwo.1 = (bf16[2,6144,128]{2,1,0:T(8,128)(2,1)}, bf16[2,128,6144]{2,1,0:T(8,128)(2,1)}, f32[2,1,6144]{2,1,0:T(1,128)}, bf16[256,2048]{1,0:T(8,128)(2,1)}) custom-call(bf16[6144,2048]{1,0:T(8,128)(2,1)} %all-gather.11.cloned.1.call-done.g_ref, bf16[2048,256]{1,0:T(8,128)(2,1)} %bitcast.43, f32[2,128,6144]{2,1,0:T(8,128)} %get-tuple-element.53.ot_ref), custom_call_target="tpu_custom_call" | custom-call | flops 12884901888 | bytes 25165824 | tf_op jit(solution)/shard_map/do_dwo/pallas_call | solution.py:183
  281.5 0.2 all-gather.17.cloned.1.call-start
  281.7 60.7 %attn_bwd.2 = bf16[6144,384]{1,0:T(8,128)(2,1)} custom-call(bf16[2,6144,128]{2,1,0:T(8,128)(2,1)} %get-tuple-element.42.k_ref, bf16[2,6144,128]{2,1,0:T(8,128)(2,1)} %get-tuple-element.48.v_ref, bf16[2,128,6144]{2,1,0:T(8,128)(2,1)} %get-tuple-element.49.kt_ref, bf16[2,6144,128]{2,1,0:T(8,128)(2,1)} %get-tuple-element.50.q_ref, ...), custom_call_target="tpu_custom_call" | custom-call | flops 48318382080 | bytes 15728640 | tf_op jit(solution)/shard_map/attn_bwd/pallas_call | solution.py:251
  342.4 20.2 %convolution_convert_fusion.1 = bf16[2048,384]{1,0:T(8,128)(2,1)} fusion(bf16[6144,2048]{1,0:T(8,128)(2,1)} %all-gather.9.cloned.1.call-done.h_ref, bf16[6144,384]{1,0:T(8,128)(2,1)} %attn_bwd.2), kind=kOutput, calls=%fused_computation.19 | convolution fusion | flops 9664462848 | bytes 31457280 | tf_op jit(solution)/shard_map/td,te->de/dot_general | solution.py:341
  362.6 0.3 all-gather.15.cloned.1.call-start
  362.8 60.6 %attn_bwd.3 = bf16[6144,384]{1,0:T(8,128)(2,1)} custom-call(bf16[2,6144,128]{2,1,0:T(8,128)(2,1)} %get-tuple-element.42.k_ref, bf16[2,6144,128]{2,1,0:T(8,128)(2,1)} %get-tuple-element.48.v_ref, bf16[2,128,6144]{2,1,0:T(8,128)(2,1)} %get-tuple-element.49.kt_ref, bf16[2,6144,128]{2,1,0:T(8,128)(2,1)} %get-tuple-element.50.q_ref, ...), custom_call_target="tpu_custom_call" | custom-call | flops 48318382080 | bytes 15728640 | tf_op jit(solution)/shard_map/attn_bwd/pallas_call | solution.py:251
  423.5 20.4 %convolution_convert_fusion.2 = bf16[2048,384]{1,0:T(8,128)(2,1)} fusion(bf16[6144,2048]{1,0:T(8,128)(2,1)} %all-gather.9.cloned.1.call-done.h_ref, bf16[6144,384]{1,0:T(8,128)(2,1)} %attn_bwd.3), kind=kOutput, calls=%fused_computation.20 | convolution fusion | flops 9664462848 | bytes 31457280 | tf_op jit(solution)/shard_map/td,te->de/dot_general | solution.py:341
  443.9 58.1 %all_to_all.15 = bf16[8,768,256]{2,1,0:T(8,128)(2,1)} all-to-all(bf16[8,768,256]{2,1,0:T(8,128)(2,1)S(1)} %bitcast.41), channel_id=1, replica_groups=mesh['dp'=2,'sp'=8] {'sp'}, dimensions={0} | all-to-all | bytes 6291456 | tf_op jit(solution)/shard_map/all_to_all | solution.py:327
  502.1 90.0 %all_to_all.16 = bf16[8,768,384]{2,1,0:T(8,128)(2,1)} all-to-all(bf16[8,768,384]{2,1,0:T(8,128)(2,1)S(1)} %bitcast.38), channel_id=1, replica_groups=mesh['dp'=2,'sp'=8] {'sp'}, dimensions={0} | all-to-all | bytes 9437184 | tf_op jit(solution)/shard_map/all_to_all | solution.py:327
  592.1 5.3 all-to-all-start.1
  597.4 0.5 convert_reduce_fusion
  597.9 1.0 fusion.4
  598.8 4.6 copy.38
  603.5 12.0 %convolution_convert_fusion = bf16[768,2048]{1,0:T(8,128)(2,1)} fusion(bf16[768,2048]{0,1:T(8,128)(2,1)} %bitcast.42, bf16[2048,2048]{1,0:T(8,128)(2,1)} %param.15), kind=kOutput, calls=%fused_computation.16 | convolution fusion | flops 6444023808 | bytes 14680064 | tf_op jit(solution)/shard_map/dot_general | solution.py:64
  615.4 6.6 copy.40
  622.1 30.0 %all-to-all-done.1 = bf16[8,768,384]{2,1,0:T(8,128)(2,1)} async-done(((bf16[8,768,384]{2,1,0:T(8,128)(2,1)}), bf16[8,768,384]{2,1,0:T(8,128)(2,1)}, u32[]{:S(2)}, u32[]{:S(2)}) %all-to-all-start.1) | async-done | bytes 4718624 | tf_op jit(solution)/shard_map/all_to_all | solution.py:327
  652.1 6.6 copy.39
  658.7 14.9 %fusion.16 = f32[768,2048]{1,0:T(8,128)S(1)} fusion(bf16[768,3072]{0,1:T(8,128)(2,1)} %bitcast.40, bf16[2048,3072]{0,1:T(8,128)(2,1)} %bitcast.33), kind=kOutput, calls=%fused_computation.40 | convolution fusion | flops 9663676416 | bytes 23592960 | tf_op jit(solution)/shard_map/te,de->td/dot_general | solution.py:343
  673.6 16.8 %fusion.7 = (f32[2048]{0:T(1024)S(1)}, f32[768]{0:T(1024)S(1)}, f32[768,2048]{1,0:T(8,128)}) fusion(bf16[768,2048]{1,0:T(8,128)(2,1)S(1)} %copy-done, f32[768]{0:T(1024)S(1)} %fusion.9, f32[768]{0:T(1024)S(1)} %broadcast_multiply_fusion, f32[2048]{0:T(1024)S(1)} %convert_element_type.34, f32[768,2048]{1,0:T(8,128)S(1)} %fusion.16, ...), kind=kOutput, calls=%fused_computation.11 | convolution fusion | flops 9677829120 | bytes 33055744 | tf_op jit(solution)/shard_map/te,de->td/dot_general | solution.py:343
  690.4 12.7 %psum.7 = bf16[2048]{0:T(1024)(128)(2,1)} all-reduce(f32[2048]{0:T(1024)S(1)} %get-tuple-element.67), channel_id=1, replica_groups=mesh['dp'=2,'sp'=8] {'sp'}, use_global_device_ids=true, to_apply=%region_5.6 | all-reduce | flops 2048 | bytes 12288 | tf_op jit(solution)/shard_map/psum | solution.py:349
  703.1 4.1 fusion.14
  707.2 2.1 add_convert_fusion
  709.3 8.9 %copy_rows.1 = bf16[2048,2048]{1,0:T(8,128)(2,1)} custom-call(bf16[2048,2048]{1,0:T(8,128)(2,1)} %all-gather.13.cloned.1.call-done.a_ref), custom_call_target="tpu_custom_call" | custom-call | flops 4194304 | bytes 16777216 | tf_op jit(solution)/shard_map/copy_rows/pallas_call | solution.py:270
  718.2 11.9 %place.2 = (bf16[2048,2048]{1,0:T(8,128)(2,1)}, bf16[2048,2048]{1,0:T(8,128)(2,1)}, bf16[2048,2048]{1,0:T(8,128)(2,1)}) custom-call(bf16[8,2048,384]{2,1,0:T(8,128)(2,1)} %bitcast.34), custom_call_target="tpu_custom_call" | custom-call | flops 6291456 | bytes 25165824 | tf_op jit(solution)/shard_map/place/pallas_call | solution.py:286
  730.2 12.0 %place.3 = (bf16[2048,2048]{1,0:T(8,128)(2,1)}, bf16[2048,2048]{1,0:T(8,128)(2,1)}, bf16[2048,2048]{1,0:T(8,128)(2,1)}) custom-call(bf16[8,2048,384]{2,1,0:T(8,128)(2,1)} %bitcast.36, bf16[2048,2048]{1,0:T(8,128)(2,1)} %get-tuple-element.60.refs_0_, ...), custom_call_target="tpu_custom_call", output_to_operand_aliasing={{0}: (1, {}), {1}: (2, {}), {2}: (3, {})} | custom-call | flops 6291456 | bytes 25165824 | tf_op jit(solution)/shard_map/place/pallas_call | solution.py:286
  (28 shorter events, 0.2 us)
Async XLA Ops:
  7.2 6.6 copy-start.5
  7.2 130.9 %all-gather.9.cloned.1.call-start = ((), (), s32[]{:S(2)}) async-start(), calls=%async_computation.3 | async-start | bytes 28311552 | tf_op jit(solution)/shard_map/all_gather | solution.py:310
  13.7 247.7 %all-gather.11.cloned.1.call-start = ((), (), s32[]{:S(2)}) async-start(), calls=%async_computation.4 | async-start | bytes 28311552 | tf_op jit(solution)/shard_map/all_gather | solution.py:319
  138.1 571.2 %all-gather.13.cloned.1.call-start = ((), (), s32[]{:S(2)}) async-start(), calls=%async_computation.5 | async-start | bytes 9437184 | tf_op jit(solution)/shard_map/all_gather | solution.py:333
  281.5 436.7 %all-gather.17.cloned.1.call-start = ((), (), s32[]{:S(2)}) async-start(), calls=%async_computation.7 | async-start | bytes 14155776 | tf_op jit(solution)/shard_map/all_gather | solution.py:342
  362.6 367.6 %all-gather.15.cloned.1.call-start = ((), (), s32[]{:S(2)}) async-start(), calls=%async_computation.6 | async-start | bytes 14155776 | tf_op jit(solution)/shard_map/all_gather | solution.py:342
  423.5 20.4 %copy-start.3 = (bf16[6144,256]{1,0:T(8,128)(2,1)S(1)}, bf16[6144,256]{1,0:T(8,128)(2,1)}, u32[]{:S(2)}) copy-start(bf16[6144,256]{1,0:T(8,128)(2,1)} %get-tuple-element.47) | copy-start | bytes 9437188
  443.9 58.2 %copy-start.1 = (bf16[6144,384]{1,0:T(8,128)(2,1)S(1)}, bf16[6144,384]{1,0:T(8,128)(2,1)}, u32[]{:S(2)}) copy-start(bf16[6144,384]{1,0:T(8,128)(2,1)} %attn_bwd.3) | copy-start | bytes 14155780
  592.0 5.3 copy-start.4
  592.1 5.3 copy-start
  592.1 60.0 %all-to-all-start.1 = ((bf16[8,768,384]{2,1,0:T(8,128)(2,1)}), bf16[8,768,384]{2,1,0:T(8,128)(2,1)}, u32[]{:S(2)}, u32[]{:S(2)}) async-start(bf16[8,768,384]{2,1,0:T(8,128)(2,1)} %bitcast.37), calls=%async_computation.1 | async-start | bytes 9437184 | tf_op jit(solution)/shard_map/all_to_all | solution.py:327
  658.7 14.9 %copy-start.2 = (bf16[768,8,384]{0,2,1:T(8,128)(2,1)S(1)}, bf16[768,8,384]{0,2,1:T(8,128)(2,1)}, u32[]{:S(2)}) copy-start(bf16[768,8,384]{0,2,1:T(8,128)(2,1)} %copy.40) | copy-start | bytes 14155780
Sparse Core Ops, SparseCore 0:
  13.8 124.2 all-gather.8
  139.9 121.4 all-gather.10
  281.6 50.5 all-gather.12
  362.7 68.2 all-gather.16
  444.0 147.8 all-gather.14

commit v3 on v2

--- a/solution.py
+++ b/solution.py
@@ -41,6 +41,102 @@
         out_shape=jax.ShapeDtypeStruct((rows, feat), BF16),
         cost_estimate=pl.CostEstimate(flops=10 * rows * feat, bytes_accessed=4 * rows * feat, transcendentals=rows),
     )(hidden, weight[None, :])
+
+
+def gather_kernel(h_ref, pos_ref, all_ref, pos_all_ref, send, recv, psend, precv, lsem):
+    me = lax.axis_index('sp')
+    rows = h_ref.shape[0]
+    half = rows // 2
+    core, x_pos, y_pos = lax.rem(me, 2), lax.rem(me // 2, 2), me // 4
+    d_x, d_y, d_c = 2 - 4 * x_pos, 4 - 8 * y_pos, 1 - 2 * core
+    x_nbr, y_nbr, c_nbr = me + d_x, me + d_y, me + d_c
+    diag = me + d_x + d_y
+
+    barrier = pltpu.get_barrier_semaphore()
+    for r in range(1, 8):
+        pl.semaphore_signal(barrier, inc=1, device_id={'sp': lax.rem(me + r, 8)}, device_id_type=pl.DeviceIdType.MESH)
+    pl.semaphore_wait(barrier, 7)
+
+    def region(owner, part):
+        return all_ref.at[pl.ds(pl.multiple_of(owner * rows + part * half, half), half)]
+
+    def copy(k, src, owner, part, dst):
+        return pltpu.make_async_remote_copy(src_ref=src, dst_ref=region(owner, part), send_sem=send.at[k], recv_sem=recv.at[k],
+                                            device_id={'sp': dst}, device_id_type=pl.DeviceIdType.MESH)
+
+    def own(part):
+        return h_ref.at[pl.ds(part * half, half)]
+
+    pos_copies = []
+    for r in range(1, 8):
+        cp = pltpu.make_async_remote_copy(src_ref=pos_ref, dst_ref=pos_all_ref.at[me], send_sem=psend.at[r - 1], recv_sem=precv.at[r - 1],
+                                          device_id={'sp': lax.rem(me + r, 8)}, device_id_type=pl.DeviceIdType.MESH)
+        cp.start()
+        pos_copies.append(cp)
+    sends = {}
+
+    def start(k, src, owner, part, dst):
+        sends[k] = copy(k, src, owner, part, dst)
+        sends[k].start()
+
+    def arrived(k, owner, part):
+        copy(k, region(owner, part), owner, part, me).wait_recv()
+
+    start(0, own(0), me, 0, x_nbr)
+    start(3, own(1), me, 1, y_nbr)
+    start(1, own(1), me, 1, x_nbr)
+    start(2, own(0), me, 0, y_nbr)
+    start(4, own(0), me, 0, c_nbr)
+    start(5, own(1), me, 1, c_nbr)
+    local = [pltpu.make_async_copy(h_ref, all_ref.at[pl.ds(pl.multiple_of(me * rows, rows), rows)], lsem.at[0]),
+             pltpu.make_async_copy(pos_ref, pos_all_ref.at[me], lsem.at[1])]
+    for cp in local:
+        cp.start()
+    arrived(0, x_nbr, 0)
+    start(6, region(x_nbr, 0), x_nbr, 0, y_nbr)
+    start(8, region(x_nbr, 0), x_nbr, 0, c_nbr)
+    arrived(3, y_nbr, 1)
+    start(7, region(y_nbr, 1), y_nbr, 1, x_nbr)
+    start(11, region(y_nbr, 1), y_nbr, 1, c_nbr)
+    arrived(1, x_nbr, 1)
+    start(9, region(x_nbr, 1), x_nbr, 1, c_nbr)
+    arrived(2, y_nbr, 0)
+    start(10, region(y_nbr, 0), y_nbr, 0, c_nbr)
+    arrived(6, diag, 0)
+    start(12, region(diag, 0), diag, 0, c_nbr)
+    arrived(7, diag, 1)
+    start(13, region(diag, 1), diag, 1, c_nbr)
+    arrived(4, c_nbr, 0)
+    arrived(5, c_nbr, 1)
+    arrived(8, x_nbr + d_c, 0)
+    arrived(9, x_nbr + d_c, 1)
+    arrived(10, y_nbr + d_c, 0)
+    arrived(11, y_nbr + d_c, 1)
+    arrived(12, diag + d_c, 0)
+    arrived(13, diag + d_c, 1)
+    for cp in list(sends.values()) + pos_copies:
+        cp.wait_send()
+    for r in range(1, 8):
+        src = lax.rem(me + 8 - r, 8)
+        pltpu.make_async_remote_copy(src_ref=pos_all_ref.at[src], dst_ref=pos_all_ref.at[src], send_sem=psend.at[r - 1],
+                                     recv_sem=precv.at[r - 1], device_id={'sp': me}, device_id_type=pl.DeviceIdType.MESH).wait_recv()
+    for cp in local:
+        cp.wait()
+
+
+def gather_tokens(normed, positions):
+    rows, feat = normed.shape
+    pos_pad = jnp.pad(positions, (0, 1024 - rows)).reshape(8, 128)
+    h_all, pos_all = pl.pallas_call(
+        gather_kernel, name='gather_tokens',
+        in_specs=[pl.BlockSpec(memory_space=pltpu.VMEM)] * 2, out_specs=[pl.BlockSpec(memory_space=pl.ANY)] * 2,
+        out_shape=[jax.ShapeDtypeStruct((8 * rows, feat), BF16), jax.ShapeDtypeStruct((8, 8, 128), jnp.int32)],
+        scratch_shapes=[pltpu.SemaphoreType.DMA((14,)), pltpu.SemaphoreType.DMA((14,)), pltpu.SemaphoreType.DMA((7,)),
+                        pltpu.SemaphoreType.DMA((7,)), pltpu.SemaphoreType.DMA((2,))],
+        compiler_params=pltpu.CompilerParams(collective_id=3, has_side_effects=True, vmem_limit_bytes=VLIM),
+        cost_estimate=pl.CostEstimate(flops=0, bytes_accessed=16 * rows * feat, transcendentals=0),
+    )(normed, pos_pad)
+    return h_all, pos_all.reshape(8, 1024)[:, :rows].reshape(-1)
 
 
 def rope_tables(positions):
@@ -260,6 +356,144 @@
     )(k, v, k_t, q, q_t, d_o, d_ot, lse, dsum, cos_t, sin_t)
 
 
+def dw_kernel(h_ref, g_ref, out_ref, acc_ref):
+    step = pl.program_id(0)
+    feat = h_ref.shape[1]
+    tile = math.gcd(feat, 512)
+
+    @pl.when(step == 0)
+    def _():
+        acc_ref[...] = jnp.zeros_like(acc_ref)
+
+    def body(i, carry):
+        cols = pl.ds(pl.multiple_of(i * tile, tile), tile)
+        acc_ref[:, cols] += lax.dot_general(g_ref[...], h_ref[:, cols], (((0,), (0,)), ((), ())), preferred_element_type=F32)
+        return carry
+
+    lax.fori_loop(0, feat // tile, body, 0)
+
+    @pl.when(step == pl.num_programs(0) - 1)
+    def _():
+        def flip(i, carry):
+            rows = pl.ds(pl.multiple_of(i * tile, tile), tile)
+            out_ref[rows, :] = acc_ref[:, rows].astype(BF16).T
+            return carry
+
+        lax.fori_loop(0, feat // tile, flip, 0)
+
+
+def weight_grad(h_all, g_tok):
+    rows, feat = h_all.shape
+    width = g_tok.shape[1]
+    bm = math.gcd(rows, 1024)
+    return pl.pallas_call(
+        dw_kernel, grid=(rows // bm,), name='weight_grad',
+        in_specs=[pl.BlockSpec((bm, feat), lambda i: (i, 0)), pl.BlockSpec((bm, width), lambda i: (i, 0))],
+        out_specs=pl.BlockSpec((feat, width), lambda i: (0, 0)), out_shape=jax.ShapeDtypeStruct((feat, width), BF16),
+        scratch_shapes=[pltpu.VMEM((width, feat), F32)],
+        compiler_params=pltpu.CompilerParams(vmem_limit_bytes=VLIM),
+        cost_estimate=pl.CostEstimate(flops=2 * rows * feat * width, bytes_accessed=2 * rows * feat, transcendentals=0),
+    )(h_all, g_tok)
+
+
+def out_kernel(o_ref, w_ref, out_ref, acc_ref):
+    step = pl.program_id(0)
+    tile = math.gcd(w_ref.shape[1], 512)
+
+    @pl.when(step == 0)
+    def _():
+        acc_ref[...] = jnp.zeros_like(acc_ref)
+
+    def body(i, carry):
+        cols = pl.ds(pl.multiple_of(i * tile, tile), tile)
+        acc_ref[:, cols] += dot_f32(o_ref[0], w_ref[:, cols])
+        return carry
+
+    lax.fori_loop(0, w_ref.shape[1] // tile, body, 0)
+
+    @pl.when(step == pl.num_programs(0) - 1)
+    def _():
+        out_ref[...] = acc_ref[...].astype(BF16)
+
+
+def out_proj(o_own, w_o):
+    devs, rows, width = o_own.shape
+    feat = w_o.shape[1]
+    return pl.pallas_call(
+        out_kernel, grid=(devs,), name='out_proj',
+        in_specs=[pl.BlockSpec((1, rows, width), lambda j: (j, 0, 0)), pl.BlockSpec((width, feat), lambda j: (j, 0))],
+        out_specs=pl.BlockSpec((rows, feat), lambda j: (0, 0)), out_shape=jax.ShapeDtypeStruct((rows, feat), BF16),
+        scratch_shapes=[pltpu.VMEM((rows, feat), F32)],
+        compiler_params=pltpu.CompilerParams(vmem_limit_bytes=VLIM),
+        cost_estimate=pl.CostEstimate(flops=2 * devs * rows * feat * width, bytes_accessed=2 * devs * feat * width, transcendentals=0),
+    )(o_own, w_o)
+
+
+def dh_kernel(heads, *refs):
+    g_refs, w_refs = refs[:heads], refs[heads:heads + 3]
+    x_ref, lnw_ref, dx_ref, dlnw_ref, acc_ref = refs[heads + 3:]
+    step = pl.program_id(0)
+    rows, feat = acc_ref.shape
+    tile = math.gcd(feat, 512)
+
+    @pl.when(step == 0)
+    def _():
+        acc_ref[...] = jnp.zeros_like(acc_ref)
+        dlnw_ref[...] = jnp.zeros_like(dlnw_ref)
+
+    def body(i, carry):
+        cols = pl.ds(pl.multiple_of(i * tile, tile), tile)
+        total = acc_ref[:, cols]
+        for idx in range(3):
+            lanes = slice(idx * HEAD_DIM, (idx + 1) * HEAD_DIM)
+            lhs = jnp.concatenate([g_ref[0, :, lanes] for g_ref in g_refs], axis=1)
+            total += lax.dot_general(lhs, w_refs[idx][cols, :], (((1,), (1,)), ((), ())), preferred_element_type=F32)
+        acc_ref[:, cols] = total
+        return carry
+
+    lax.fori_loop(0, feat // tile, body, 0)
+
+    @pl.when(step == pl.num_programs(0) - 1)
+    def _():
+        bm = math.gcd(rows, 64)
+        weight = lnw_ref[...].astype(F32)
+
+        def norm_bwd(i, carry):
+            own = pl.ds(pl.multiple_of(i * bm, bm), bm)
+            hid = x_ref[own, :].astype(F32)
+            d_h = acc_ref[own, :]
+            centered = hid - jnp.mean(hid, axis=-1, keepdims=True)
+            rstd = lax.rsqrt(jnp.mean(centered * centered, axis=-1, keepdims=True) + LN_EPS)
+            x_hat = centered * rstd
+            dlnw_ref[...] += jnp.sum(d_h * x_hat, axis=0, keepdims=True)
+            d_hat = d_h * weight
+            mean_d = jnp.mean(d_hat, axis=-1, keepdims=True)
+            mean_dx = jnp.mean(d_hat * x_hat, axis=-1, keepdims=True)
+            dx_ref[own, :] = (rstd * (d_hat - mean_d - x_hat * mean_dx)).astype(BF16)
+            return carry
+
+        lax.fori_loop(0, rows // bm, norm_bwd, 0)
+
+
+def hidden_grad(g_owns, weights, hidden, ln_weight):
+    devs, rows, width = g_owns[0].shape
+    heads = len(g_owns)
+    feat = hidden.shape[1]
+    whole = pl.BlockSpec((rows, feat), lambda j: (0, 0))
+    vec = pl.BlockSpec((1, feat), lambda j: (0, 0))
+    return pl.pallas_call(
+        functools.partial(dh_kernel, heads), grid=(devs,), name='hidden_grad',
+        in_specs=[pl.BlockSpec((1, rows, width), lambda j: (j, 0, 0))] * heads
+        + [pl.BlockSpec((feat, heads * HEAD_DIM), lambda j: (0, j))] * 3 + [whole, vec],
+        out_specs=[whole, vec],
+        out_shape=[jax.ShapeDtypeStruct((rows, feat), BF16), jax.ShapeDtypeStruct((1, feat), F32)],
+        scratch_shapes=[pltpu.VMEM((rows, feat), F32)],
+        compiler_params=pltpu.CompilerParams(vmem_limit_bytes=VLIM),
+        cost_estimate=pl.CostEstimate(flops=2 * devs * heads * rows * feat * width, bytes_accessed=6 * feat * feat,
+                                      transcendentals=rows),
+    )(*g_owns, *weights, hidden, ln_weight[None, :])
+
+
 def copy_kernel(a_ref, out_ref):
     out_ref[...] = a_ref[...]
 
@@ -301,20 +535,16 @@
     grad_spec = P('dp', None)
 
     def layer_step(hidden, positions, d_attn, ln_weight, w_q, w_k, w_v, w_o):
-        feat, all_width = w_q.shape
+        _, all_width = w_q.shape
         width = all_width // sp_size
         heads = width // HEAD_DIM
         me = lax.axis_index('sp')
         normed = layer_norm(hidden, ln_weight)
-        pos_all = lax.all_gather(positions, 'sp', axis=0, tiled=True)
-        h_all = lax.all_gather(normed, 'sp', axis=0, tiled=True)
+        h_all, pos_all = gather_tokens(normed, positions)
         cos_t, sin_t = rope_tables(pos_all)
         own = lambda w: lax.dynamic_slice_in_dim(w, me * width, width, 1)
         w_cat = jnp.concatenate([own(w_q), own(w_k), own(w_v)], axis=1)
         wo_cols = lax.dynamic_slice_in_dim(w_o, me * width, width, 0).T
-        stacked = jnp.stack([w.reshape(feat, sp_size, heads, HEAD_DIM) for w in (w_q, w_k, w_v)], axis=3)
-        w_slot = [stacked[:, :, n].reshape(feat, sp_size * 3 * HEAD_DIM) for n in range(heads)]
-        h_all, cos_t, sin_t, w_cat, wo_cols, w_slot = lax.optimization_barrier((h_all, cos_t, sin_t, w_cat, wo_cols, w_slot))
         g_dep, h_all = lax.optimization_barrier((d_attn, h_all))
         g_all = lax.all_gather(g_dep, 'sp', axis=0, tiled=True)
         q, k, v, q_t, k_t, v_t = project(h_all, w_cat, cos_t, sin_t, heads)
@@ -325,29 +555,27 @@
         def to_owner(val):
             val = with_layout_constraint(val.reshape(sp_size, -1, val.shape[1]), row_major)
             val = with_layout_constraint(lax.all_to_all(val, 'sp', 0, 0, tiled=True), row_major)
-            return val.transpose(1, 0, 2).reshape(val.shape[1], -1)
+            return val
 
         o_tok, g_all = lax.optimization_barrier((o_tok, g_all))
         o_own = to_owner(o_tok)
         d_o, d_ot, dsum, dw_o = project_do(g_all, wo_cols, o_t, heads)
         dw_o = lax.all_gather(dw_o, 'sp', axis=0, tiled=True)
         dw_o = copy_rows(dw_o)
-        attn_out = dot_f32(o_own, w_o).astype(BF16)
+        attn_out = out_proj(o_own, w_o)
         d_ws = []
-        d_normed = 0.0
+        g_owns = []
         for n in range(heads):
             g_tok = attn_bwd(n, k, v, k_t, q, q_t, d_o, d_ot, lse, dsum, cos_t, sin_t)
-            g_own = to_owner(g_tok)
-            d_w = jnp.einsum('td,te->de', h_all, g_tok, preferred_element_type=F32).astype(BF16)
+            g_owns.append(to_owner(g_tok))
+            d_w = weight_grad(h_all, g_tok)
             d_ws.append(lax.all_gather(d_w, 'sp', axis=0))
-            d_normed = d_normed + jnp.einsum('te,de->td', g_own, w_slot[n], preferred_element_type=F32)
         grads = ()
         for n in range(heads):
             grads = place_slot(n, heads, d_ws[n], grads)
-        norm_vjp = jax.vjp(norm_f32, hidden.astype(F32), ln_weight.astype(F32))[1]
-        d_hid, d_lnw = norm_vjp(d_normed)
-        d_lnw = lax.psum(d_lnw, 'sp')
-        return (attn_out, d_hid.astype(BF16), d_lnw.astype(BF16), grads[0], grads[1], grads[2], dw_o)
+        d_hid, d_lnw = hidden_grad(g_owns, (w_q, w_k, w_v), hidden, ln_weight)
+        d_lnw = lax.psum(d_lnw[0], 'sp')
+        return (attn_out, d_hid, d_lnw.astype(BF16), grads[0], grads[1], grads[2], dw_o)
 
     return jax.shard_map(layer_step, mesh=mesh,
                          in_specs=(row_spec, pos_spec, row_spec, P(None), full_spec, full_spec, full_spec, full_spec),

time: 755 us -> 732 us (0.970)
  Pallas kernels: 281 us -> 487 us
  matrix products: 84.3 us -> 0 us
  local copies, waits for them, and re-layouts: 83.2 us -> 8.66 us
  other arithmetic: 42.6 us -> 15.5 us
  waiting for transfers between devices: 66 us -> 39.1 us
  blocking collectives: 172 us -> 161 us
    pallas_call x0 -> x5, Pallas kernels: none -> 207 us  [the longest x1 115 us: gather_tokens(): pl.pallas_call(gather_kernel, name='gather_tokens', in_specs=[pl.BlockSpe...]
    dot_general x5 -> x0, matrix products: 84.3 us -> none  [the longest x2 40.6 us: layer_step(): jnp.einsum('td,te->de', h_all, g_tok, preferred_element_type=F32)]
    unnamed x17 -> x8, local copies, waits for them, and re-layouts: 38.2 us -> 1.34 us
    all_gather x1, waiting for transfers between devices: 21.4 us -> 0.01 us  [layer_step(): g_all = lax.all_gather(g_dep, 'sp', axis=0, tiled=True)]
    slice x3 -> x0, local copies, waits for them, and re-layouts: 21.3 us -> none  [layer_step(): stacked[:, :, n].reshape(feat, sp_size * 3 * HEAD_DIM)]
    another operation x1 -> x0, other arithmetic: 19.6 us -> none  [layer_step(): jnp.stack([w.reshape(feat, sp_size, heads, HEAD_DIM) for w in (w_q, w_k,...]
    transpose x3 -> x0, local copies, waits for them, and re-layouts: 17.9 us -> none  [to_owner(): return val.transpose(1, 0, 2).reshape(val.shape[1], -1)]
    all_gather x1 -> x0, waiting for transfers between devices: 14.5 us -> none  [layer_step(): h_all = lax.all_gather(normed, 'sp', axis=0, tiled=True)]
  transfers between devices with their start and end apart: 6 -> 5, of which waited for: 3 -> 1; matrix products, arithmetic and copies ran while one was open for 28% -> 3% of each run, Pallas kernels for 33% -> 46%
where the time goes in v3:
time: 732 us; the launch traced here: 731 us
  Pallas kernels  487 us (67%)
  blocking collectives  161 us (22%)
  waiting for transfers between devices  39.1 us (5%)
  other arithmetic  15.5 us (2%)
  between operations  13.9 us (2%)
  local copies, waits for them, and re-layouts  8.66 us (1%)
    all_to_all x2, blocking collectives, to_owner(): lax.all_to_all(val, 'sp', 0, 0, tiled=True)  148 us
    pallas_call x2, Pallas kernels, attn_bwd(): pl.pallas_call(functools.partial(bwd_kernel, blk, n_blk), grid=(n_blk,),...  121 us
    pallas_call x1, Pallas kernels, gather_tokens(): pl.pallas_call(gather_kernel, name='gather_tokens', in_specs=[pl.BlockSpe...  115 us
    pallas_call x1, Pallas kernels, attn_fwd(): pl.pallas_call(functools.partial(fwd_kernel, blk, heads), grid=(rows // b...  69.7 us
    all_to_all x1, waiting for transfers between devices, to_owner(): lax.all_to_all(val, 'sp', 0, 0, tiled=True)  39 us
    pallas_call x2, Pallas kernels, weight_grad(): pl.pallas_call(dw_kernel, grid=(rows // bm,), name='weight_grad', in_spec...  38.1 us
    pallas_call x1, Pallas kernels, hidden_grad(): pl.pallas_call(functools.partial(dh_kernel, heads), grid=(devs,), name='h...  37.6 us
    pallas_call x1, Pallas kernels, project(): pl.pallas_call(functools.partial(proj_kernel, heads), grid=(rows // bm,),...  31.6 us
  transfers between devices with their start and end apart: 5, of which 1 were waited for; matrix products, arithmetic and copies ran while one was open for 3% of the time, Pallas kernels for 46%

profile of v3, /device:TPU:0, one launch (start us, length us, event | category | flops | bytes accessed | tf_op | source)
XLA Modules:
  0.0 730.6 jit_solution(11575105869865514379)
XLA Ops:
  7.2 0.0 all-gather.7.cloned.1.call-start
  7.2 1.3 pad_bitcast_fusion.pos_ref
  8.5 1.3 broadcast_in_dim.15.w_ref.refs_6_
  9.8 5.2 layer_norm.1.h_ref
  14.9 115.2 %gather_tokens.1 = (bf16[6144,2048]{1,0:T(8,128)(2,1)}, s32[8,8,128]{2,1,0:T(8,128)}) custom-call(bf16[768,2048]{1,0:T(8,128)(2,1)} %layer_norm.1.h_ref, s32[8,128]{1,0:T(8,128)} %pad_bitcast_fusion.pos_ref), custom_call_target="tpu_custom_call" | custom-call | bytes 25165824 | tf_op jit(solution)/shard_map/gather_tokens/pallas_call | solution.py:130
  130.1 0.0 copy-start.2
  130.1 0.0 all-gather.7.cloned.1.call-update
  130.1 0.0 all-gather.9.cloned.1.call-start
  130.2 1.3 constant_dynamic-slice_fusion
  131.5 1.3 copy.19
  132.8 0.0 copy-done.2
  132.9 1.3 constant_dynamic-slice_fusion.3
  134.2 2.2 constant_dynamic-slice_fusion.1
  136.3 1.9 pad_maximum_fusion.w_ref
  138.2 13.6 %fusion = (f32[6144,128]{1,0:T(8,128)}, f32[6144,128]{1,0:T(8,128)}) fusion(f32[128]{0:T(128)S(1)} %get-tuple-element.63, f32[128]{0:T(128)S(1)} %get-tuple-element.64, f32[6144]{0:T(1024)S(1)} %convert_element_type.21), kind=kLoop, calls=%fused_computation.2 | loop fusion | flops 1572864 | bytes 6317056 | tf_op jit(solution)/shard_map/mul | solution.py:147
  151.8 31.6 %qkv_proj.1 = (bf16[2,6144,128]{2,1,0:T(8,128)(2,1)}, bf16[2,6144,128]{2,1,0:T(8,128)(2,1)}, bf16[2,6144,128]{2,1,0:T(8,128)(2,1)}, bf16[2,128,6144]{2,1,0:T(8,1...) custom-call(bf16[6144,2048]{1,0:T(8,128)(2,1)} %get-tuple-element.35.h_ref, ...), custom_call_target="tpu_custom_call" | custom-call | flops 19327352832 | bytes 25165824 | tf_op jit(solution)/shard_map/qkv_proj/pallas_call | solution.py:186
  183.4 69.7 %attn_fwd.1 = (bf16[6144,256]{1,0:T(8,128)(2,1)}, f32[2,128,6144]{2,1,0:T(8,128)}, f32[2,1,6144]{2,1,0:T(1,128)}) custom-call(bf16[2,6144,128]{2,1,0:T(8,128)(2,1)} %get-tuple-element.37.k_ref, bf16[2,128,6144]{2,1,0:T(8,128)(2,1)} %get-tuple-element.38.qt_ref, bf16[2,128,6144]{2,1,0:T(8,128)(2,1)} %get-tuple-element.39.vt_ref), custom_call_target="tpu_custom_call" | custom-call | flops 38654705664 | bytes 12582912 | tf_op jit(solution)/shard_map/attn_fwd/pallas_call | solution.py:235
  253.1 0.0 all-gather.7.cloned.1.call-done.g_ref
  253.1 20.1 %do_dwo.1 = (bf16[2,6144,128]{2,1,0:T(8,128)(2,1)}, bf16[2,128,6144]{2,1,0:T(8,128)(2,1)}, f32[2,1,6144]{2,1,0:T(1,128)}, bf16[256,2048]{1,0:T(8,128)(2,1)}) custom-call(bf16[6144,2048]{1,0:T(8,128)(2,1)} %all-gather.7.cloned.1.call-done.g_ref, bf16[2048,256]{1,0:T(8,128)(2,1)} %bitcast.18, f32[2,128,6144]{2,1,0:T(8,128)} %get-tuple-element.47.ot_ref), custom_call_target="tpu_custom_call" | custom-call | flops 12884901888 | bytes 25165824 | tf_op jit(solution)/shard_map/do_dwo/pallas_call | solution.py:279
  273.2 0.0 all-gather.9.cloned.1.call-update
  273.2 0.2 all-gather.13.cloned.1.call-start
  273.5 60.6 %attn_bwd.2.g_ref = bf16[6144,384]{1,0:T(8,128)(2,1)} custom-call(bf16[2,6144,128]{2,1,0:T(8,128)(2,1)} %get-tuple-element.37.k_ref, bf16[2,6144,128]{2,1,0:T(8,128)(2,1)} %get-tuple-element.43.v_ref, bf16[2,128,6144]{2,1,0:T(8,128)(2,1)} %get-tuple-element.44.kt_ref, bf16[2,6144,128]{2,1,0:T(8,128)(2,1)} %get-tuple-element.45.q_ref, ...), custom_call_target="tpu_custom_call" | custom-call | flops 48318382080 | bytes 15728640 | tf_op jit(solution)/shard_map/attn_bwd/pallas_call | solution.py:347
  334.1 19.0 %weight_grad.3 = bf16[2048,384]{1,0:T(8,128)(2,1)} custom-call(bf16[6144,2048]{1,0:T(8,128)(2,1)} %get-tuple-element.35.h_ref, bf16[6144,384]{1,0:T(8,128)(2,1)} %attn_bwd.2.g_ref), custom_call_target="tpu_custom_call" | custom-call | flops 9663676416 | bytes 25165824 | tf_op jit(solution)/shard_map/weight_grad/pallas_call | solution.py:389
  353.1 0.0 all-gather.13.cloned.1.call-update
  353.1 0.0 all-gather.11.cloned.1.call-start
  353.2 60.7 %attn_bwd.3.g_ref = bf16[6144,384]{1,0:T(8,128)(2,1)} custom-call(bf16[2,6144,128]{2,1,0:T(8,128)(2,1)} %get-tuple-element.37.k_ref, bf16[2,6144,128]{2,1,0:T(8,128)(2,1)} %get-tuple-element.43.v_ref, bf16[2,128,6144]{2,1,0:T(8,128)(2,1)} %get-tuple-element.44.kt_ref, bf16[2,6144,128]{2,1,0:T(8,128)(2,1)} %get-tuple-element.45.q_ref, ...), custom_call_target="tpu_custom_call" | custom-call | flops 48318382080 | bytes 15728640 | tf_op jit(solution)/shard_map/attn_bwd/pallas_call | solution.py:347
  413.8 0.0 copy-start.1
  413.8 19.1 %weight_grad.2 = bf16[2048,384]{1,0:T(8,128)(2,1)} custom-call(bf16[6144,2048]{1,0:T(8,128)(2,1)} %get-tuple-element.35.h_ref, bf16[6144,384]{1,0:T(8,128)(2,1)} %attn_bwd.3.g_ref), custom_call_target="tpu_custom_call" | custom-call | flops 9663676416 | bytes 25165824 | tf_op jit(solution)/shard_map/weight_grad/pallas_call | solution.py:389
  432.9 0.0 all-gather.11.cloned.1.call-update
  433.0 0.0 copy-done.1
  433.0 0.0 copy-start
  433.0 58.4 %all_to_all.15.o_ref = bf16[8,768,256]{2,1,0:T(8,128)(2,1)} all-to-all(bf16[8,768,256]{2,1,0:T(8,128)(2,1)S(1)} %bitcast.17), channel_id=1, replica_groups=mesh['dp'=2,'sp'=8] {'sp'}, dimensions={0} | all-to-all | bytes 6291456 | tf_op jit(solution)/shard_map/all_to_all | solution.py:557
  491.4 0.0 copy-done
  491.4 90.0 %all_to_all.16.refs_1_ = bf16[8,768,384]{2,1,0:T(8,128)(2,1)} all-to-all(bf16[8,768,384]{2,1,0:T(8,128)(2,1)S(1)} %bitcast.16), channel_id=1, replica_groups=mesh['dp'=2,'sp'=8] {'sp'}, dimensions={0} | all-to-all | bytes 9437184 | tf_op jit(solution)/shard_map/all_to_all | solution.py:557
  581.4 4.7 all-to-all-start.1
  586.1 15.7 %out_proj.1 = bf16[768,2048]{1,0:T(8,128)(2,1)} custom-call(bf16[8,768,256]{2,1,0:T(8,128)(2,1)} %all_to_all.15.o_ref, bf16[2048,2048]{1,0:T(8,128)(2,1)} %w_ref.1), custom_call_target="tpu_custom_call" | custom-call | flops 6442450944 | bytes 8388608 | tf_op jit(solution)/shard_map/out_proj/pallas_call | solution.py:422
  601.8 39.0 %all-to-all-done.1.refs_0_ = bf16[8,768,384]{2,1,0:T(8,128)(2,1)} async-done(((bf16[8,768,384]{2,1,0:T(8,128)(2,1)}), bf16[8,768,384]{2,1,0:T(8,128)(2,1)}, u32[]{:S(2)}, u32[]{:S(2)}) %all-to-all-start.1) | async-done | bytes 4718624 | tf_op jit(solution)/shard_map/all_to_all | solution.py:557
  640.8 37.6 %hidden_grad.1 = (bf16[768,2048]{1,0:T(8,128)(2,1)}, f32[1,2048]{1,0:T(1,128)}) custom-call(bf16[8,768,384]{2,1,0:T(8,128)(2,1)} %all-to-all-done.1.refs_0_, bf16[8,768,384]{2,1,0:T(8,128)(2,1)} %all_to_all.16.refs_1_, bf16[2048,2048]{1,0:T(8,128)(2,1)} %refs_2_.1, bf16[2048,2048]{1,0:T(8,128)(2,1)} %refs_3_.1, bf16[2048,2048]{1,0:T(8,128)(2,1)} %refs_4_.1, ...), custom_call_target="tpu_custom_call" | custom-call | flops 19327352832 | bytes 25165824 | tf_op jit(solution)/shard_map/hidden_grad/pallas_call | solution.py:484
  678.4 12.8 %psum.7 = bf16[2048]{0:T(1024)(128)(2,1)} all-reduce(f32[2048]{0:T(1024)} %bitcast.21), channel_id=1, replica_groups=mesh['dp'=2,'sp'=8] {'sp'}, use_global_device_ids=true, to_apply=%region_0.1 | all-reduce | flops 2048 | bytes 12288 | tf_op jit(solution)/shard_map/psum | solution.py:577
  691.2 0.0 all-gather.9.cloned.1.call-done.a_ref
  691.2 8.9 %copy_rows.1 = bf16[2048,2048]{1,0:T(8,128)(2,1)} custom-call(bf16[2048,2048]{1,0:T(8,128)(2,1)} %all-gather.9.cloned.1.call-done.a_ref), custom_call_target="tpu_custom_call" | custom-call | flops 4194304 | bytes 16777216 | tf_op jit(solution)/shard_map/copy_rows/pallas_call | solution.py:504
  700.2 0.0 all-gather.13.cloned.1.call-done
  700.2 11.9 %place.2 = (bf16[2048,2048]{1,0:T(8,128)(2,1)}, bf16[2048,2048]{1,0:T(8,128)(2,1)}, bf16[2048,2048]{1,0:T(8,128)(2,1)}) custom-call(bf16[8,2048,384]{2,1,0:T(8,128)(2,1)} %bitcast.13), custom_call_target="tpu_custom_call" | custom-call | flops 6291456 | bytes 25165824 | tf_op jit(solution)/shard_map/place/pallas_call | solution.py:520
  712.1 0.0 all-gather.11.cloned.1.call-done
  712.1 12.0 %place.3 = (bf16[2048,2048]{1,0:T(8,128)(2,1)}, bf16[2048,2048]{1,0:T(8,128)(2,1)}, bf16[2048,2048]{1,0:T(8,128)(2,1)}) custom-call(bf16[8,2048,384]{2,1,0:T(8,128)(2,1)} %bitcast.14, bf16[2048,2048]{1,0:T(8,128)(2,1)} %get-tuple-element.54.refs_0_, ...), custom_call_target="tpu_custom_call", output_to_operand_aliasing={{0}: (1, {}), {1}: (2, {}), {2}: (3, {})} | custom-call | flops 6291456 | bytes 25165824 | tf_op jit(solution)/shard_map/place/pallas_call | solution.py:520
  (4 shorter events, 0.0 us)
Async XLA Ops:
  7.2 245.9 %all-gather.7.cloned.1.call-start = ((), (), s32[]{:S(2)}) async-start(), calls=%async_computation.3 | async-start | bytes 28311552 | tf_op jit(solution)/shard_map/all_gather | solution.py:549
  130.1 2.7 copy-start.2
  130.1 561.1 %all-gather.9.cloned.1.call-start = ((), (), s32[]{:S(2)}) async-start(), calls=%async_computation.4 | async-start | bytes 9437184 | tf_op jit(solution)/shard_map/all_gather | solution.py:563
  273.2 426.9 %all-gather.13.cloned.1.call-start = ((), (), s32[]{:S(2)}) async-start(), calls=%async_computation.6 | async-start | bytes 14155776 | tf_op jit(solution)/shard_map/all_gather | solution.py:572
  353.1 359.0 %all-gather.11.cloned.1.call-start = ((), (), s32[]{:S(2)}) async-start(), calls=%async_computation.5 | async-start | bytes 14155776 | tf_op jit(solution)/shard_map/all_gather | solution.py:572
  413.8 19.1 %copy-start.1 = (bf16[6144,256]{1,0:T(8,128)(2,1)S(1)}, bf16[6144,256]{1,0:T(8,128)(2,1)}, u32[]{:S(2)}) copy-start(bf16[6144,256]{1,0:T(8,128)(2,1)} %get-tuple-element.42) | copy-start | bytes 9437188
  433.0 58.4 %copy-start = (bf16[6144,384]{1,0:T(8,128)(2,1)S(1)}, bf16[6144,384]{1,0:T(8,128)(2,1)}, u32[]{:S(2)}) copy-start(bf16[6144,384]{1,0:T(8,128)(2,1)} %attn_bwd.3.g_ref) | copy-start | bytes 14155780
  581.4 59.4 %all-to-all-start.1 = ((bf16[8,768,384]{2,1,0:T(8,128)(2,1)}), bf16[8,768,384]{2,1,0:T(8,128)(2,1)}, u32[]{:S(2)}, u32[]{:S(2)}) async-start(bf16[8,768,384]{2,1,0:T(8,128)(2,1)} %bitcast.15), calls=%async_computation.1 | async-start | bytes 9437184 | tf_op jit(solution)/shard_map/all_to_all | solution.py:557
Sparse Core Ops, SparseCore 0:
  130.3 121.6 all-gather.6
  273.4 51.3 all-gather.8
  353.2 69.0 all-gather.12
  433.1 148.1 all-gather.10

commit v4 on v3

--- a/solution.py
+++ b/solution.py
@@ -160,11 +160,11 @@
     return jnp.dot(lhs, rhs, preferred_element_type=F32)
 
 
-def proj_kernel(heads, h_ref, w_ref, cos_ref, sin_ref, q_ref, k_ref, v_ref, qt_ref, kt_ref, vt_ref):
+def proj_kernel(heads, me_ref, h_ref, wq_ref, wk_ref, wv_ref, cos_ref, sin_ref, q_ref, k_ref, v_ref, qt_ref, kt_ref, vt_ref):
     cos_t, sin_t = cos_ref[...], sin_ref[...]
-    width = heads * HEAD_DIM
+    w_refs = (wq_ref, wk_ref, wv_ref)
     for idx, (out, out_t) in enumerate(((q_ref, qt_ref), (k_ref, kt_ref), (v_ref, vt_ref))):
-        prod = dot_f32(h_ref[...], w_ref[:, idx * width:(idx + 1) * width])
+        prod = dot_f32(h_ref[...], w_refs[idx][...])
         for n in range(heads):
             val = prod[:, n * HEAD_DIM:(n + 1) * HEAD_DIM]
             if idx < 2:
@@ -174,22 +174,25 @@
             out_t[n] = val.T
 
 
-def project(h_all, w_cat, cos_t, sin_t, heads):
+def project(me, h_all, weights, cos_t, sin_t, heads):
     rows, feat = h_all.shape
-    width = w_cat.shape[1]
+    width = heads * HEAD_DIM
     bm = math.gcd(rows, 512)
-    tok = pl.BlockSpec((heads, bm, HEAD_DIM), lambda i: (0, i, 0))
-    tr = pl.BlockSpec((heads, HEAD_DIM, bm), lambda i: (0, 0, i))
-    tab = pl.BlockSpec((bm, HEAD_DIM), lambda i: (i, 0))
+    tok = pl.BlockSpec((heads, bm, HEAD_DIM), lambda i, m: (0, i, 0))
+    tr = pl.BlockSpec((heads, HEAD_DIM, bm), lambda i, m: (0, 0, i))
+    tab = pl.BlockSpec((bm, HEAD_DIM), lambda i, m: (i, 0))
+    own = pl.BlockSpec((feat, width), lambda i, m: (0, m[0]))
     s_tok = jax.ShapeDtypeStruct((heads, rows, HEAD_DIM), BF16)
     s_tr = jax.ShapeDtypeStruct((heads, HEAD_DIM, rows), BF16)
     return pl.pallas_call(
-        functools.partial(proj_kernel, heads), grid=(rows // bm,), name='qkv_proj',
-        in_specs=[pl.BlockSpec((bm, feat), lambda i: (i, 0)), pl.BlockSpec((feat, width), lambda i: (0, 0)), tab, tab],
-        out_specs=[tok] * 3 + [tr] * 3, out_shape=[s_tok] * 3 + [s_tr] * 3,
-        compiler_params=pltpu.CompilerParams(vmem_limit_bytes=VLIM),
-        cost_estimate=pl.CostEstimate(flops=2 * rows * feat * width, bytes_accessed=2 * rows * feat, transcendentals=0),
-    )(h_all, w_cat, cos_t, sin_t)
+        functools.partial(proj_kernel, heads), name='qkv_proj', out_shape=[s_tok] * 3 + [s_tr] * 3,
+        grid_spec=pltpu.PrefetchScalarGridSpec(
+            num_scalar_prefetch=1, grid=(rows // bm,),
+            in_specs=[pl.BlockSpec((bm, feat), lambda i, m: (i, 0)), own, own, own, tab, tab],
+            out_specs=[tok] * 3 + [tr] * 3),
+        compiler_params=pltpu.CompilerParams(vmem_limit_bytes=VLIM),
+        cost_estimate=pl.CostEstimate(flops=6 * rows * feat * width, bytes_accessed=2 * rows * feat, transcendentals=0),
+    )(me[None], h_all, *weights, cos_t, sin_t)
 
 
 def fwd_kernel(blk, heads, k_ref, qt_ref, vt_ref, o_ref, ot_ref, lse_ref, acc_ref):
@@ -542,12 +545,10 @@
         normed = layer_norm(hidden, ln_weight)
         h_all, pos_all = gather_tokens(normed, positions)
         cos_t, sin_t = rope_tables(pos_all)
-        own = lambda w: lax.dynamic_slice_in_dim(w, me * width, width, 1)
-        w_cat = jnp.concatenate([own(w_q), own(w_k), own(w_v)], axis=1)
         wo_cols = lax.dynamic_slice_in_dim(w_o, me * width, width, 0).T
         g_dep, h_all = lax.optimization_barrier((d_attn, h_all))
         g_all = lax.all_gather(g_dep, 'sp', axis=0, tiled=True)
-        q, k, v, q_t, k_t, v_t = project(h_all, w_cat, cos_t, sin_t, heads)
+        q, k, v, q_t, k_t, v_t = project(me, h_all, (w_q, w_k, w_v), cos_t, sin_t, heads)
         o_tok, o_t, lse = attn_fwd(k, q_t, v_t)
 
         row_major = Layout(major_to_minor=(0, 1, 2))
@@ -567,13 +568,16 @@
         g_owns = []
         for n in range(heads):
             g_tok = attn_bwd(n, k, v, k_t, q, q_t, d_o, d_ot, lse, dsum, cos_t, sin_t)
+            d_w = weight_grad(h_all, g_tok)
+            if n == heads - 1:
+                g_tok, d_w = lax.optimization_barrier((g_tok, d_w))
             g_owns.append(to_owner(g_tok))
-            d_w = weight_grad(h_all, g_tok)
             d_ws.append(lax.all_gather(d_w, 'sp', axis=0))
-        grads = ()
-        for n in range(heads):
+        grads = place_slot(0, heads, d_ws[0], ())
+        d_hid, d_lnw = hidden_grad(g_owns, (w_q, w_k, w_v), hidden, ln_weight)
+        d_hid, d_ws[1:] = lax.optimization_barrier((d_hid, d_ws[1:]))
+        for n in range(1, heads):
             grads = place_slot(n, heads, d_ws[n], grads)
-        d_hid, d_lnw = hidden_grad(g_owns, (w_q, w_k, w_v), hidden, ln_weight)
         d_lnw = lax.psum(d_lnw[0], 'sp')
         return (attn_out, d_hid, d_lnw.astype(BF16), grads[0], grads[1], grads[2], dw_o)
 

time: 732 us -> 730 us (level)
  transfers between devices with their start and end apart: 5 -> 5, of which waited for: 1 -> 2; matrix products, arithmetic and copies ran while one was open for 3% -> 2% of each run, Pallas kernels for 46% -> 44%
where the time goes in v4:
time: 730 us; the launch traced here: 729 us
  Pallas kernels  488 us (67%)
  blocking collectives  161 us (22%)
  waiting for transfers between devices  42.5 us (6%)
  between operations  13.9 us (2%)
  other arithmetic  13.7 us (2%)
    all_to_all x2, blocking collectives, to_owner(): lax.all_to_all(val, 'sp', 0, 0, tiled=True)  148 us
    pallas_call x2, Pallas kernels, attn_bwd(): pl.pallas_call(functools.partial(bwd_kernel, blk, n_blk), grid=(n_blk,),...  121 us
    pallas_call x1, Pallas kernels, gather_tokens(): pl.pallas_call(gather_kernel, name='gather_tokens', in_specs=[pl.BlockSpe...  115 us
    pallas_call x1, Pallas kernels, attn_fwd(): pl.pallas_call(functools.partial(fwd_kernel, blk, heads), grid=(rows // b...  70.6 us
    all_to_all x1, waiting for transfers between devices, to_owner(): lax.all_to_all(val, 'sp', 0, 0, tiled=True)  39.1 us
    pallas_call x2, Pallas kernels, weight_grad(): pl.pallas_call(dw_kernel, grid=(rows // bm,), name='weight_grad', in_spec...  38.2 us
    pallas_call x1, Pallas kernels, hidden_grad(): pl.pallas_call(functools.partial(dh_kernel, heads), grid=(devs,), name='h...  37.6 us
    pallas_call x1, Pallas kernels, project(): pl.pallas_call(functools.partial(proj_kernel, heads), name='qkv_proj', ou...  31.5 us
  transfers between devices with their start and end apart: 5, of which 2 were waited for; matrix products, arithmetic and copies ran while one was open for 2% of the time, Pallas kernels for 44%

profile of v4, /device:TPU:0, one launch (start us, length us, event | category | flops | bytes accessed | tf_op | source)
XLA Modules:
  0.0 729.4 jit_solution(9694551158715510393)
XLA Ops:
  7.2 0.0 all-gather.7.cloned.1.call-start
  7.2 1.3 pad_bitcast_fusion.pos_ref
  8.5 1.3 broadcast_in_dim.19.w_ref.refs_6_
  9.8 5.2 layer_norm.1.h_ref
  14.9 115.2 %gather_tokens.1 = (bf16[6144,2048]{1,0:T(8,128)(2,1)}, s32[8,8,128]{2,1,0:T(8,128)}) custom-call(bf16[768,2048]{1,0:T(8,128)(2,1)} %layer_norm.1.h_ref, s32[8,128]{1,0:T(8,128)} %pad_bitcast_fusion.pos_ref), custom_call_target="tpu_custom_call" | custom-call | bytes 25165824 | tf_op jit(solution)/shard_map/gather_tokens/pallas_call | solution.py:130
  130.1 0.0 copy-start.2
  130.1 0.0 all-gather.7.cloned.1.call-update
  130.1 0.0 all-gather.9.cloned.1.call-start
  130.2 1.3 constant_dynamic-slice_fusion
  131.5 1.3 copy.19
  132.8 0.0 copy-done.2
  132.9 13.6 %fusion = (f32[6144,128]{1,0:T(8,128)}, f32[6144,128]{1,0:T(8,128)}) fusion(f32[128]{0:T(128)S(1)} %get-tuple-element.71, f32[128]{0:T(128)S(1)} %get-tuple-element.72, f32[6144]{0:T(1024)S(1)} %convert_element_type.21), kind=kLoop, calls=%fused_computation.2 | loop fusion | flops 1572864 | bytes 6317056 | tf_op jit(solution)/shard_map/mul | solution.py:147
  146.5 31.5 %qkv_proj.1 = (bf16[2,6144,128]{2,1,0:T(8,128)(2,1)}, bf16[2,6144,128]{2,1,0:T(8,128)(2,1)}, bf16[2,6144,128]{2,1,0:T(8,128)(2,1)}, bf16[2,128,6144]{2,1,0:T(8,1...) custom-call(s32[1]{0:T(128)} %bitcast.me_ref, bf16[6144,2048]{1,0:T(8,128)(2,1)} %get-tuple-element.39.h_ref, ...), custom_call_target="tpu_custom_call" | custom-call | flops 19327352832 | bytes 25165824 | tf_op jit(solution)/shard_map/qkv_proj/pallas_call | solution.py:187
  178.0 70.6 %attn_fwd.1 = (bf16[6144,256]{1,0:T(8,128)(2,1)}, f32[2,128,6144]{2,1,0:T(8,128)}, f32[2,1,6144]{2,1,0:T(1,128)}) custom-call(bf16[2,6144,128]{2,1,0:T(8,128)(2,1)} %get-tuple-element.41.k_ref, bf16[2,128,6144]{2,1,0:T(8,128)(2,1)} %get-tuple-element.42.qt_ref, bf16[2,128,6144]{2,1,0:T(8,128)(2,1)} %get-tuple-element.43.vt_ref), custom_call_target="tpu_custom_call" | custom-call | flops 38654705664 | bytes 12582912 | tf_op jit(solution)/shard_map/attn_fwd/pallas_call | solution.py:238
  248.6 3.3 all-gather.7.cloned.1.call-done.g_ref
  251.9 20.0 %do_dwo.1 = (bf16[2,6144,128]{2,1,0:T(8,128)(2,1)}, bf16[2,128,6144]{2,1,0:T(8,128)(2,1)}, f32[2,1,6144]{2,1,0:T(1,128)}, bf16[256,2048]{1,0:T(8,128)(2,1)}) custom-call(bf16[6144,2048]{1,0:T(8,128)(2,1)} %all-gather.7.cloned.1.call-done.g_ref, bf16[2048,256]{1,0:T(8,128)(2,1)} %bitcast.19, f32[2,128,6144]{2,1,0:T(8,128)} %get-tuple-element.51.ot_ref), custom_call_target="tpu_custom_call" | custom-call | flops 12884901888 | bytes 25165824 | tf_op jit(solution)/shard_map/do_dwo/pallas_call | solution.py:282
  272.0 0.0 all-gather.9.cloned.1.call-update
  272.0 0.2 all-gather.11.cloned.1.call-start
  272.2 60.7 %attn_bwd.3.g_ref = bf16[6144,384]{1,0:T(8,128)(2,1)} custom-call(bf16[2,6144,128]{2,1,0:T(8,128)(2,1)} %get-tuple-element.41.k_ref, bf16[2,6144,128]{2,1,0:T(8,128)(2,1)} %get-tuple-element.47.v_ref, bf16[2,128,6144]{2,1,0:T(8,128)(2,1)} %get-tuple-element.48.kt_ref, bf16[2,6144,128]{2,1,0:T(8,128)(2,1)} %get-tuple-element.49.q_ref, ...), custom_call_target="tpu_custom_call" | custom-call | flops 48318382080 | bytes 15728640 | tf_op jit(solution)/shard_map/attn_bwd/pallas_call | solution.py:350
  332.9 19.0 %weight_grad.2 = bf16[2048,384]{1,0:T(8,128)(2,1)} custom-call(bf16[6144,2048]{1,0:T(8,128)(2,1)} %get-tuple-element.39.h_ref, bf16[6144,384]{1,0:T(8,128)(2,1)} %attn_bwd.3.g_ref), custom_call_target="tpu_custom_call" | custom-call | flops 9663676416 | bytes 25165824 | tf_op jit(solution)/shard_map/weight_grad/pallas_call | solution.py:392
  351.9 0.0 all-gather.11.cloned.1.call-update
  351.9 0.3 all-gather.13.cloned.1.call-start
  352.1 60.7 %attn_bwd.2.g_ref = bf16[6144,384]{1,0:T(8,128)(2,1)} custom-call(bf16[2,6144,128]{2,1,0:T(8,128)(2,1)} %get-tuple-element.41.k_ref, bf16[2,6144,128]{2,1,0:T(8,128)(2,1)} %get-tuple-element.47.v_ref, bf16[2,128,6144]{2,1,0:T(8,128)(2,1)} %get-tuple-element.48.kt_ref, bf16[2,6144,128]{2,1,0:T(8,128)(2,1)} %get-tuple-element.49.q_ref, ...), custom_call_target="tpu_custom_call" | custom-call | flops 48318382080 | bytes 15728640 | tf_op jit(solution)/shard_map/attn_bwd/pallas_call | solution.py:350
  412.8 0.0 copy-start.1
  412.8 19.3 %weight_grad.3 = bf16[2048,384]{1,0:T(8,128)(2,1)} custom-call(bf16[6144,2048]{1,0:T(8,128)(2,1)} %get-tuple-element.39.h_ref, bf16[6144,384]{1,0:T(8,128)(2,1)} %attn_bwd.2.g_ref), custom_call_target="tpu_custom_call" | custom-call | flops 9663676416 | bytes 25165824 | tf_op jit(solution)/shard_map/weight_grad/pallas_call | solution.py:392
  432.1 0.0 all-gather.13.cloned.1.call-update
  432.1 0.0 copy-done.1
  432.1 0.0 copy-start
  432.1 58.1 %all_to_all.15.o_ref = bf16[8,768,256]{2,1,0:T(8,128)(2,1)} all-to-all(bf16[8,768,256]{2,1,0:T(8,128)(2,1)S(1)} %bitcast.18), channel_id=1, replica_groups=mesh['dp'=2,'sp'=8] {'sp'}, dimensions={0} | all-to-all | bytes 6291456 | tf_op jit(solution)/shard_map/all_to_all | solution.py:558
  490.2 0.0 copy-done
  490.2 90.0 %all_to_all.16.refs_0_ = bf16[8,768,384]{2,1,0:T(8,128)(2,1)} all-to-all(bf16[8,768,384]{2,1,0:T(8,128)(2,1)S(1)} %bitcast.17), channel_id=1, replica_groups=mesh['dp'=2,'sp'=8] {'sp'}, dimensions={0} | all-to-all | bytes 9437184 | tf_op jit(solution)/shard_map/all_to_all | solution.py:558
  580.2 4.7 all-to-all-start.2
  584.9 15.6 %out_proj.1 = bf16[768,2048]{1,0:T(8,128)(2,1)} custom-call(bf16[8,768,256]{2,1,0:T(8,128)(2,1)} %all_to_all.15.o_ref, bf16[2048,2048]{1,0:T(8,128)(2,1)} %w_ref.1), custom_call_target="tpu_custom_call" | custom-call | flops 6442450944 | bytes 8388608 | tf_op jit(solution)/shard_map/out_proj/pallas_call | solution.py:425
  600.5 39.1 %all-to-all-done.2.refs_1_ = bf16[8,768,384]{2,1,0:T(8,128)(2,1)} async-done(((bf16[8,768,384]{2,1,0:T(8,128)(2,1)}), bf16[8,768,384]{2,1,0:T(8,128)(2,1)}, u32[]{:S(2)}, u32[]{:S(2)}) %all-to-all-start.2) | async-done | bytes 4718624 | tf_op jit(solution)/shard_map/all_to_all | solution.py:558
  639.6 37.6 %hidden_grad.1 = (bf16[768,2048]{1,0:T(8,128)(2,1)}, f32[1,2048]{1,0:T(1,128)}) custom-call(bf16[8,768,384]{2,1,0:T(8,128)(2,1)} %all_to_all.16.refs_0_, bf16[8,768,384]{2,1,0:T(8,128)(2,1)} %all-to-all-done.2.refs_1_, bf16[2048,2048]{1,0:T(8,128)(2,1)} %refs_2_.1, bf16[2048,2048]{1,0:T(8,128)(2,1)} %refs_3_.1, bf16[2048,2048]{1,0:T(8,128)(2,1)} %refs_4_.1, ...), custom_call_target="tpu_custom_call" | custom-call | flops 19327352832 | bytes 25165824 | tf_op jit(solution)/shard_map/hidden_grad/pallas_call | solution.py:487
  677.2 12.8 %psum.7 = bf16[2048]{0:T(1024)(128)(2,1)} all-reduce(f32[2048]{0:T(1024)} %bitcast.22), channel_id=1, replica_groups=mesh['dp'=2,'sp'=8] {'sp'}, use_global_device_ids=true, to_apply=%region_0.1 | all-reduce | flops 2048 | bytes 12288 | tf_op jit(solution)/shard_map/psum | solution.py:581
  690.0 0.0 all-gather.9.cloned.1.call-done.a_ref
  690.0 8.9 %copy_rows.1 = bf16[2048,2048]{1,0:T(8,128)(2,1)} custom-call(bf16[2048,2048]{1,0:T(8,128)(2,1)} %all-gather.9.cloned.1.call-done.a_ref), custom_call_target="tpu_custom_call" | custom-call | flops 4194304 | bytes 16777216 | tf_op jit(solution)/shard_map/copy_rows/pallas_call | solution.py:507
  698.9 0.0 all-gather.11.cloned.1.call-done
  698.9 0.0 all-gather.13.cloned.1.call-done
  699.0 12.0 %place.2 = (bf16[2048,2048]{1,0:T(8,128)(2,1)}, bf16[2048,2048]{1,0:T(8,128)(2,1)}, bf16[2048,2048]{1,0:T(8,128)(2,1)}) custom-call(bf16[8,2048,384]{2,1,0:T(8,128)(2,1)} %bitcast.14), custom_call_target="tpu_custom_call" | custom-call | flops 6291456 | bytes 25165824 | tf_op jit(solution)/shard_map/place/pallas_call | solution.py:523
  710.9 11.9 %place.3 = (bf16[2048,2048]{1,0:T(8,128)(2,1)}, bf16[2048,2048]{1,0:T(8,128)(2,1)}, bf16[2048,2048]{1,0:T(8,128)(2,1)}) custom-call(bf16[8,2048,384]{2,1,0:T(8,128)(2,1)} %bitcast.15, bf16[2048,2048]{1,0:T(8,128)(2,1)} %get-tuple-element.62.refs_0_, ...), custom_call_target="tpu_custom_call", output_to_operand_aliasing={{0}: (1, {}), {1}: (2, {}), {2}: (3, {})} | custom-call | flops 6291456 | bytes 25165824 | tf_op jit(solution)/shard_map/place/pallas_call | solution.py:523
  (4 shorter events, 0.0 us)
Async XLA Ops:
  7.2 244.8 %all-gather.7.cloned.1.call-start = ((), (), s32[]{:S(2)}) async-start(), calls=%async_computation.3 | async-start | bytes 28311552 | tf_op jit(solution)/shard_map/all_gather | solution.py:550
  130.1 2.7 copy-start.2
  130.1 559.9 %all-gather.9.cloned.1.call-start = ((), (), s32[]{:S(2)}) async-start(), calls=%async_computation.4 | async-start | bytes 9437184 | tf_op jit(solution)/shard_map/all_gather | solution.py:564
  272.0 427.0 %all-gather.11.cloned.1.call-start = ((), (), s32[]{:S(2)}) async-start(), calls=%async_computation.5 | async-start | bytes 14155776 | tf_op jit(solution)/shard_map/all_gather | solution.py:575
  351.9 347.1 %all-gather.13.cloned.1.call-start = ((), (), s32[]{:S(2)}) async-start(), calls=%async_computation.6 | async-start | bytes 14155776 | tf_op jit(solution)/shard_map/all_gather | solution.py:575
  412.8 19.3 %copy-start.1 = (bf16[6144,256]{1,0:T(8,128)(2,1)S(1)}, bf16[6144,256]{1,0:T(8,128)(2,1)}, u32[]{:S(2)}) copy-start(bf16[6144,256]{1,0:T(8,128)(2,1)} %get-tuple-element.46) | copy-start | bytes 9437188
  432.1 58.2 %copy-start = (bf16[6144,384]{1,0:T(8,128)(2,1)S(1)}, bf16[6144,384]{1,0:T(8,128)(2,1)}, u32[]{:S(2)}) copy-start(bf16[6144,384]{1,0:T(8,128)(2,1)} %attn_bwd.2.g_ref) | copy-start | bytes 14155780
  580.2 59.4 %all-to-all-start.2 = ((bf16[8,768,384]{2,1,0:T(8,128)(2,1)}), bf16[8,768,384]{2,1,0:T(8,128)(2,1)}, u32[]{:S(2)}, u32[]{:S(2)}) async-start(bf16[8,768,384]{2,1,0:T(8,128)(2,1)} %bitcast.16), calls=%async_computation.2 | async-start | bytes 9437184 | tf_op jit(solution)/shard_map/all_to_all | solution.py:558
Sparse Core Ops, SparseCore 0:
  130.3 121.6 all-gather.6
  272.1 50.4 all-gather.8
  352.0 68.2 all-gather.10
  432.2 147.8 all-gather.12
